TPU v7x, 128 devices: a whole 4x4x4 slice. The times are simulated.
128 devices in a mesh: tp: 8 (over z_hi, x), seq: 16 (over y, z_lo, core).
Axes of the slice: x: 4, y: 4, z: 4 (z_hi: 2, z_lo: 2; z = z_hi * 2 + z_lo), core: 2. Of those that a mesh axis runs over, the one named last changes fastest.
Arguments:
- query_rows: bfloat16 [4096, 8192], P('seq', 'tp'), may hold values from -24 to 24
- key_rows: bfloat16 [4096, 1024], P('seq', 'tp'), may hold values from -9 to 9
- value_rows: bfloat16 [4096, 1024], P('seq', 'tp'), may hold values from -9 to 9
- mixer_input: bfloat16 [4096, 8192], P('seq', 'tp'), may hold values from -6 to 6
- write_rows: bfloat16 [4096, 128], P('seq'), may hold values from -48 to 48
- read_rows: bfloat16 [4096, 128], P('seq'), may hold values from -48 to 48
- log_step: float32 [128, 4096], P('tp', 'seq'), may hold values from -20 to -4
- log_decay: float32 [128, 4096], P('tp', 'seq'), may hold values from -2 to 0
Outputs:
- grad_input: float32 [4096, 8192], P('seq', 'tp')
- grad_write: float32 [4096, 128], P('seq')
- grad_read: float32 [4096, 128], P('seq')
- grad_log_step: float32 [128, 4096], P('tp', 'seq')
All inputs are finite; a program needn't handle non-finite values.
Results may differ from a plain program's by a relative error of at most 0.0015.
Values may be sent and summed in bfloat16 or wider, within the bound.
A program may use at most 128 MiB of HBM per device.

v0:
```python
import math

import jax
import jax.numpy as jnp
from jax import lax
from jax.sharding import PartitionSpec as P

BLOCK = 128
HD = 128


precise = lax.Precision.HIGHEST


def in_one_piece(arrays, axis, dim, along):
    widths = [a.shape[along] for a in arrays]
    both = jnp.concatenate(arrays, axis=along)
    filled = lax.all_gather(both, axis, axis=dim, tiled=True)
    return tuple(jnp.split(filled, [sum(widths[:k]) for k in range(1, len(widths))], axis=along))


def prefix(value, axis, join, neutral, backward):
    count, mine = (lax.axis_size(axis), lax.axis_index(axis))
    pieces = jax.tree.map(lambda part: lax.all_gather(part, axis), value)
    if backward:
        pieces = jax.tree.map(lambda part: part[::-1], pieces)
        mine = count - 1 - mine
    subtotal = jax.tree.map(
        lambda part, zero: jnp.full_like(part, 0) + jnp.asarray(zero, part.dtype), value, neutral
    )

    def hop(position, subtotal):
        longer = join(subtotal, jax.tree.map(lambda part: part[position], pieces))
        return jax.tree.map(lambda new, old: jnp.where(position < mine, new, old), longer, subtotal)

    return lax.fori_loop(0, count - 1, hop, subtotal)


def sent_to_all(array, axis):
    devices = lax.axis_size(axis)
    return lax.all_to_all(
        jnp.broadcast_to(array[None], (devices, *array.shape)), axis, 0, 0, tiled=True
    )


def taken_together(array, axis):
    return sent_to_all(array, axis).sum(axis=0)


def together(arrays, axis):
    ends = [0]
    for a in arrays:
        ends.append(ends[-1] + a.size)
    subtotal = taken_together(jnp.concatenate([a.ravel() for a in arrays]), axis)
    return tuple((subtotal[b:e].reshape(a.shape) for a, b, e in zip(arrays, ends, ends[1:])))


def combine(earlier, later):
    return (earlier[0] * later[0], later[0][:, None, None] * earlier[1] + later[1])


def teacher_attention(query_rows, key_rows, value_rows):
    tok_count = query_rows.shape[0]
    local_kv = key_rows.shape[1] // HD
    members = query_rows.shape[1] // (local_kv * HD)
    grouped = query_rows.reshape(tok_count, local_kv, members, HD)
    query_pos = lax.axis_index("seq") * tok_count + jnp.arange(tok_count, dtype=jnp.int32)
    scaling = 1.0 / math.sqrt(HD)
    stats_shape = (local_kv, members, tok_count)
    pieces = in_one_piece((key_rows, value_rows), "seq", 0, 1)
    run_max = jnp.full(stats_shape, -1e30, jnp.float32)
    row_count = pieces[0].shape[0]
    key_heads = pieces[0].reshape(row_count, local_kv, HD)
    value_heads = pieces[1].reshape(row_count, local_kv, HD)
    scores = (
        jnp.einsum("igrd,jgd->grij", grouped, key_heads, preferred_element_type=jnp.float32)
        * scaling
    )
    key_pos = jnp.arange(row_count, dtype=jnp.int32)
    allowed = key_pos[None, :] <= query_pos[:, None]
    scores = jnp.where(allowed, scores, -1e30)
    new_max = jnp.maximum(run_max, jnp.max(scores, axis=-1))
    weights = jnp.where(allowed, jnp.exp(scores - new_max[..., None]), 0.0)
    new_sum = jnp.sum(weights, axis=-1)
    update = jnp.einsum(
        "grij,jgd->igrd",
        weights.astype(jnp.bfloat16),
        value_heads,
        preferred_element_type=jnp.float32,
    )
    output = update / jnp.transpose(new_sum, (2, 0, 1))[..., None]
    return output.reshape(tok_count, local_kv * members * HD).astype(jnp.bfloat16)


def on_device(
    query_rows, key_rows, value_rows, mixer_input, write_rows, read_rows, log_step, log_decay
):
    teacher = teacher_attention(query_rows, key_rows, value_rows)
    head_count, tok_count = log_step.shape
    blocks = tok_count // BLOCK
    head_width = mixer_input.shape[1] // head_count
    states = write_rows.shape[1]
    signal = mixer_input.astype(jnp.float32).reshape(blocks, BLOCK, head_count, head_width)
    writes = write_rows.astype(jnp.float32).reshape(blocks, BLOCK, states)
    reads = read_rows.astype(jnp.float32).reshape(blocks, BLOCK, states)
    step_size = jnp.exp(log_step).reshape(head_count, blocks, BLOCK)
    cum_decay = jnp.cumsum(log_decay.reshape(head_count, blocks, BLOCK), axis=-1)
    block_total = cum_decay[..., -1]
    to_end = jnp.transpose(jnp.exp(block_total[..., None] - cum_decay), (1, 2, 0))
    from_start = jnp.transpose(jnp.exp(cum_decay), (1, 2, 0))
    step_rows = jnp.transpose(step_size, (1, 2, 0))
    log_gap = cum_decay[..., :, None] - cum_decay[..., None, :]
    causal = (
        jnp.arange(BLOCK, dtype=jnp.int32)[:, None] >= jnp.arange(BLOCK, dtype=jnp.int32)[None, :]
    )
    within = jnp.where(causal, jnp.exp(jnp.where(causal, log_gap, 0.0)), 0.0)
    inner_rows = jnp.einsum("cin,cjn->cij", reads, writes, precision=precise)
    mixing = within * inner_rows[None]
    scaled = signal * step_rows[..., None]
    y_local = jnp.einsum("hcij,cjhp->cihp", mixing, scaled, precision=precise)
    block_state = jnp.einsum(
        "cjhp,cjn->chpn", scaled * to_end[..., None], writes, precision=precise
    )
    block_decay = jnp.exp(block_total)
    zeros_state = jnp.zeros((head_count, head_width, states), jnp.float32)

    def advance(running, element):
        return (element[0][:, None, None] * running + element[1], running)

    device_state, entering = lax.scan(advance, zeros_state, (block_decay.T, block_state))
    device_decay = jnp.exp(jnp.sum(block_total, axis=1))
    incoming = prefix(
        (device_decay, device_state),
        "seq",
        combine,
        (jnp.ones_like(device_decay), zeros_state),
        False,
    )[1]
    before = jnp.exp(jnp.cumsum(block_total, axis=1) - block_total)
    state_in = before.T[:, :, None, None] * incoming[None] + entering
    y_carried = (
        jnp.einsum("chpn,cin->cihp", state_in, reads, precision=precise) * from_start[..., None]
    )
    residual = (
        y_local
        + y_carried
        - teacher.astype(jnp.float32).reshape(blocks, BLOCK, head_count, head_width)
    )
    weighted = residual * from_start[..., None]
    block_adjoint = jnp.einsum("cihp,cin->chpn", weighted, reads, precision=precise)
    device_adjoint, leaving = lax.scan(
        advance, zeros_state, (block_decay.T, block_adjoint), reverse=True
    )
    arriving = prefix(
        (device_decay, device_adjoint),
        "seq",
        combine,
        (jnp.ones_like(device_decay), zeros_state),
        True,
    )[1]
    after = jnp.exp(jnp.sum(block_total, axis=1, keepdims=True) - jnp.cumsum(block_total, axis=1))
    adjoint = after.T[:, :, None, None] * arriving[None] + leaving
    back_rows = jnp.einsum("hcij,cihp->cjhp", mixing, residual, precision=precise) + to_end[
        ..., None
    ] * jnp.einsum("chpn,cjn->cjhp", adjoint, writes, precision=precise)
    grad_input = (back_rows * step_rows[..., None]).reshape(tok_count, head_count * head_width)
    grad_log_step = jnp.transpose(
        step_rows * jnp.sum(signal * back_rows, axis=-1), (2, 0, 1)
    ).reshape(head_count, tok_count)
    pair_terms = jnp.einsum("hcij,cihp,cjhp->cij", within, residual, scaled, precision=precise)
    grad_write = jnp.einsum(
        "chpn,cjhp->cjn", adjoint, scaled * to_end[..., None], precision=precise
    ) + jnp.einsum("cij,cin->cjn", pair_terms, reads, precision=precise)
    grad_read = jnp.einsum("chpn,cihp->cin", state_in, weighted, precision=precise) + jnp.einsum(
        "cij,cjn->cin", pair_terms, writes, precision=precise
    )
    grad_write, grad_read = together(
        (grad_write.reshape(tok_count, states), grad_read.reshape(tok_count, states)), "tp"
    )
    return (grad_input, grad_write, grad_read, grad_log_step)


def solution(mesh):
    in_specs = (
        P("seq", "tp"),
        P("seq", "tp"),
        P("seq", "tp"),
        P("seq", "tp"),
        P("seq", None),
        P("seq", None),
        P("tp", "seq"),
        P("tp", "seq"),
    )
    out_specs = (P("seq", "tp"), P("seq", None), P("seq", None), P("tp", "seq"))
    return jax.shard_map(
        on_device, mesh=mesh, in_specs=in_specs, out_specs=out_specs, check_vma=False
    )
```

profile of v0, /device:TPU:0, one launch (start us, length us, event | category | flops | bytes accessed | tf_op | source)
XLA Modules:
  0.0 266.6 jit_solution(17585725687352393908)
XLA Ops:
  9.7 2.8 %reshape.153 = f32[2,128,16,64]{3,2,1,0:T(8,128)} reshape(bf16[256,1024]{1,0:T(8,128)(2,1)} %param.19) | data formatting | bytes 1572864 | tf_op jit(solution)/shard_map/reshape | solution.py:103
  12.4 2.3 copy.71
  21.7 31.2 %all-reduce = f32[256]{0:T(256)S(1)} all-reduce(f32[256]{0:T(256)S(1)} %exponential_dynamic-update-slice_fusion), channel_id=2, replica_groups=mesh['tp'=8,'seq'=16] {'seq'}, use_global_device_ids=true, to_apply=%add | all-reduce | flops 256 | bytes 2048
  54.9 15.4 %fusion.4 = (f32[8,256]{1,0:T(8,128)S(1)}, f32[4096,256,8]{1,0,2:T(8,128)}) fusion(pred[256,4096]{0,1:T(8,128)(4,1)} %iota_compare_fusion, bf16[4096,256]{1,0:T(8,128)(2,1)} %all-gather.7.cloned.1.call-done, bf16[256,1024]{1,0:T(8,128)(2,1)S(1)} %copy-done), kind=kOutput, calls=%fused_computation.16 | convolution fusion | flops 2172647424 | bytes 36184064 | tf_op jit(solution)/shard_map/igrd,jgd->grij/dot_general | solution.py:76
  70.3 15.5 %fusion.5 = f32[8,256]{1,0:T(8,128)S(1)} fusion(f32[4096,256,8]{1,0,2:T(8,128)} %get-tuple-element.476, f32[8,256]{1,0:T(8,128)S(1)} %broadcast_maximum_fusion, pred[256,4096]{0,1:T(8,128)(4,1)S(1)} %copy-done.9), kind=kLoop, calls=%fused_computation.17 | loop fusion | flops 41940992 | bytes 34619392 | tf_op jit(solution)/shard_map/reduce_sum | solution.py:84
  85.8 15.9 %fusion.57 = f32[256,1,8,128]{0,3,2,1:T(8,128)} fusion(f32[4096,256,8]{1,0,2:T(8,128)} %get-tuple-element.476, f32[8,256]{1,0:T(8,128)S(1)} %broadcast_maximum_fusion, pred[256,4096]{0,1:T(8,128)(4,1)S(1)} %copy-done.9, bf16[4096,256]{1,0:T(8,128)(2,1)S(1)} %copy-done.14, f32[256,8]{0,1:T(8,128)S(1)} %bitcast.224), kind=kOutput, calls=%fused_computation.67 | convolution fusion | flops 2190213120 | bytes 36716544 | tf_op jit(solution)/shard_map/grij,jgd->igrd/dot_general | solution.py:85
  101.7 2.7 %reshape.134 = f32[2,128,16,64]{1,0,3,2:T(2,128)} reshape(f32[256,1,8,128]{0,3,2,1:T(8,128)} %fusion.57) | data formatting | bytes 2097152 | tf_op jit(solution)/shard_map/convert_element_type | solution.py:147
  104.4 18.4 %while.59 = (s32[]{:T(128)}, f32[16,64,128]{2,1,0:T(8,128)S(1)}, s32[]{:T(128)}, f32[16,16]{1,0:T(8,128)S(1)}, f32[16,16,64,128]{3,2,1,0:T(8,128)}, /*index=5*/s32[]{:T(128)}, s32[]{:T(128)}) while((s32[]{:T(128)}, f32[16,64,128]{2,1,0:T(8,128)S(1)}, s32[]{:T(128)}, f32[16,16]{1,0:T(8,128)S(1)}, f32[16,16,64,128]{3,2,1,0:T(8,128)}, ...), condition=%wide.region_6.7_spmd.clone, body=%wide.region_5.6_spmd.clone.sunk | while | flops 524292 | bytes 1573161 | solution.py:36
  122.8 2.0 fusion.31
  124.8 4.3 %fusion.35 = f32[2,128,16,64]{1,3,2,0:T(8,128)S(1)} fusion(f32[2,128,16,64]{1,3,2,0:T(8,128)S(1)} %fusion.31, f32[2,128,16,64]{1,0,3,2:T(2,128)S(1)} %copy-done.12, f32[2,128,128]{2,1,0:T(8,128)S(1)} %fusion.89, f32[16,2,128]{2,0,1:T(8,128)S(1)} %reduce_window_sum.25, pred[128,128]{1,0:T(8,128)(4,1)S(1)} %iota_compare_fusion.1, ...), kind=kOutput, calls=%fused_computation.39 | convolution fusion | flops 405536768 | bytes 4374528 | tf_op jit(solution)/shard_map/hcij,cjhp->cihp/dot_general | solution.py:120
  132.8 4.0 %while.60 = (s32[]{:T(128)}, f32[16,64,128]{2,1,0:T(8,128)S(1)}, f32[2,16,64,128]{3,2,1,0:T(8,128)}, f32[2,16]{1,0:T(2,128)S(1)}, f32[2,16,64,128]{3,2,1,0:T(8,128)}, /*index=5*/s32[]{:T(128)}, s32[]{:T(128)}) while((s32[]{:T(128)}, f32[16,64,128]{2,1,0:T(8,128)S(1)}, f32[2,16,64,128]{3,2,1,0:T(8,128)}, f32[2,16]{1,0:T(2,128)S(1)}, ...), condition=%wide.region_10.11_spmd.clone, body=%wide.region_9.10_spmd.clone.sunk | while | flops 524292 | bytes 2621744 | solution.py:151
  139.4 3.0 %copy.94 = f32[2,128,128,16]{1,2,3,0:T(8,128)} copy(f32[2,128,128,16]{2,1,3,0:T(8,128)} %fusion.12) | data formatting | bytes 4194304
  142.4 3.3 %convolution_bitcast_fusion.2 = f32[2,128,128]{2,1,0:T(8,128)S(1)} fusion(f32[2,128,16,64]{1,3,2,0:T(8,128)} %copy-done.6, f32[2,16,64,128]{3,2,1,0:T(8,128)S(1)} %copy-done.4, f32[2,128,16]{1,2,0:T(8,128)S(1)} %get-tuple-element.470, f32[16,64,128]{2,1,0:T(8,128)S(1)} %get-tuple-element.325, f32[2,16]{1,0:T(2,128)S(1)} %get-tuple-element.473), kind=kOutput, calls=%fused_computation.42 | convolution fusion | flops 403439616 | bytes 2769024 | tf_op jit(solution)/shard_map/chpn,cihp->cin/dot_general | solution.py:174
  145.7 5.1 %fusion.11 = f32[2,128,128]{1,2,0:T(8,128)S(1)} fusion(f32[2,128,128,16]{1,2,3,0:T(8,128)} %copy.94, f32[2,128,16,64]{1,3,2,0:T(8,128)S(1)} %copy-done.7, f32[2,128,16,64]{1,3,2,0:T(8,128)S(1)} %copy.71, f32[2,128,16]{1,2,0:T(8,128)S(1)} %copy.70), kind=kOutput, calls=%fused_computation.24 | convolution fusion | flops 403931136 | bytes 4341760 | tf_op jit(solution)/shard_map/hcij,cihp,cjhp->cij/dot_general | solution.py:170
  151.1 38.1 %all-gather.11.cloned.1.call-done = f32[256,64,128]{2,1,0:T(8,128)} async-done(((f32[16,64,128]{2,1,0:T(8,128)}), f32[256,64,128]{2,1,0:T(8,128)}) %all-gather.11.cloned.1.call-update) | async-done | bytes 8388624 | tf_op jit(solution)/shard_map/all_gather | solution.py:24
  189.2 8.3 %rev.7 = f32[16,16,64,128]{3,2,1,0:T(8,128)} reverse(f32[16,16,64,128]{3,2,1,0:T(8,128)} %bitcast.210), dimensions={0} | reverse | bytes 16777216 | tf_op jit(solution)/shard_map/rev | solution.py:26
  197.5 18.5 %while.61 = (s32[]{:T(128)}, f32[16,64,128]{2,1,0:T(8,128)S(1)}, s32[]{:T(128)}, f32[16,16]{1,0:T(8,128)S(1)}, f32[16,16,64,128]{3,2,1,0:T(8,128)}, /*index=5*/s32[]{:T(128)}, s32[]{:T(128)}) while((s32[]{:T(128)}, f32[16,64,128]{2,1,0:T(8,128)S(1)}, s32[]{:T(128)}, f32[16,16]{1,0:T(8,128)S(1)}, f32[16,16,64,128]{3,2,1,0:T(8,128)}, ...), condition=%wide.region_12.13_spmd.clone, body=%wide.region_11.12_spmd.clone.sunk | while | flops 524292 | bytes 1573161 | solution.py:36
  218.2 2.4 broadcast_in_dim.79
  220.6 6.7 %all-to-all-start = ((f32[8,1,65536]{2,1,0:T(1,128)}), f32[8,1,65536]{2,1,0:T(1,128)}, u32[]{:S(2)}, u32[]{:S(2)}) async-start(f32[8,1,65536]{2,1,0:T(1,128)} %broadcast_in_dim.79), calls=%async_computation | async-start | bytes 4194304 | tf_op jit(solution)/shard_map/all_to_all | solution.py:41
  228.5 2.5 multiply_reduce_fusion
  231.0 2.1 copy.98
  233.0 2.8 %reshape.152 = f32[256,1024]{1,0:T(8,128)} reshape(f32[2,128,16,64]{3,2,1,0:T(8,128)} %copy.98) | data formatting | bytes 2097152
  236.5 19.8 %all-to-all-done = f32[8,1,65536]{2,1,0:T(1,128)} async-done(((f32[8,1,65536]{2,1,0:T(1,128)}), f32[8,1,65536]{2,1,0:T(1,128)}, u32[]{:S(2)}, u32[]{:S(2)}) %all-to-all-start) | async-done | bytes 2097184 | tf_op jit(solution)/shard_map/all_to_all | solution.py:41
  256.2 3.1 %reduce_sum.47 = f32[65536]{0:T(1024)S(1)} reduce(f32[8,1,65536]{2,1,0:T(1,128)} %all-to-all-done, f32[]{:T(128)} %constant.110.clone.1), dimensions={0,1}, to_apply=%region_13.14 | reduce | flops 458752 | bytes 2359300 | tf_op jit(solution)/shard_map/reduce_sum | solution.py:47
  (149 shorter events, 63.3 us)
Async XLA Ops:
  7.2 47.7 %copy-start = (bf16[256,1024]{1,0:T(8,128)(2,1)S(1)}, bf16[256,1024]{1,0:T(8,128)(2,1)}, u32[]{:S(2)}) copy-start(bf16[256,1024]{1,0:T(8,128)(2,1)} %param.16) | copy-start | bytes 1572868
  7.2 47.7 %all-gather.7.cloned.1.call-start = ((), (), s32[]{:S(2)}) async-start(), calls=%async_computation.1 | async-start | bytes 2228224 | tf_op jit(solution)/shard_map/all_gather | solution.py:18
  8.8 95.5 %all-gather.9.cloned.1.call-start = ((), (), s32[]{:S(2)}) async-start(), calls=%async_computation.2 | async-start | bytes 8912896 | tf_op jit(solution)/shard_map/all_gather | solution.py:24
  12.4 2.4 copy-start.13
  12.4 3.3 %copy-start.11 = (bf16[256,128]{1,0:T(8,128)(2,1)S(1)}, bf16[256,128]{1,0:T(8,128)(2,1)}, u32[]{:S(2)}) copy-start(bf16[256,128]{1,0:T(8,128)(2,1)} %param.20) | copy-start | bytes 196612
  17.5 2.9 %copy-start.15 = (u32[128]{0:T(128)S(1)}, u32[128]{0:T(128)}, u32[]{:S(2)}) copy-start(u32[128]{0:T(128)} %constant.120) | copy-start | bytes 1540
  17.5 35.5 %copy-start.10 = (bf16[256,128]{1,0:T(8,128)(2,1)S(1)}, bf16[256,128]{1,0:T(8,128)(2,1)}, u32[]{:S(2)}) copy-start(bf16[256,128]{1,0:T(8,128)(2,1)} %param.21) | copy-start | bytes 196612
  19.5 0.8 copy-start.3
  20.3 168.9 %all-gather.11.cloned.1.call-start = ((), (), s32[]{:S(2)}) async-start(), calls=%async_computation.3 | async-start | bytes 8912896 | tf_op jit(solution)/shard_map/all_gather | solution.py:24
  54.9 15.4 %copy-start.9 = (pred[256,4096]{0,1:T(8,128)(4,1)S(1)}, pred[256,4096]{0,1:T(8,128)(4,1)}, u32[]{:S(2)}) copy-start(pred[256,4096]{0,1:T(8,128)(4,1)} %iota_compare_fusion) | copy-start | bytes 3145732
  70.3 15.5 %copy-start.14 = (bf16[4096,256]{1,0:T(8,128)(2,1)S(1)}, bf16[4096,256]{1,0:T(8,128)(2,1)}, u32[]{:S(2)}) copy-start(bf16[4096,256]{1,0:T(8,128)(2,1)} %all-gather.7.cloned.1.call-done) | copy-start | bytes 6291460
  122.8 2.0 copy-start.12
  129.1 1.0 copy-start.6
  136.8 0.8 copy-start.2
  139.4 3.0 %copy-start.4 = (f32[2,16,64,128]{3,2,1,0:T(8,128)S(1)}, f32[2,16,64,128]{3,2,1,0:T(8,128)}, u32[]{:S(2)}) copy-start(f32[2,16,64,128]{3,2,1,0:T(8,128)} %get-tuple-element.326) | copy-start | bytes 3145732
  142.4 3.3 %copy-start.7 = (f32[2,128,16,64]{1,3,2,0:T(8,128)S(1)}, f32[2,128,16,64]{1,3,2,0:T(8,128)}, u32[]{:S(2)}) copy-start(f32[2,128,16,64]{1,3,2,0:T(8,128)} %copy-done.6) | copy-start | bytes 3145732
  197.5 18.5 %copy-start.5 = (f32[2,16,64,128]{3,2,1,0:T(8,128)S(1)}, f32[2,16,64,128]{3,2,1,0:T(8,128)}, u32[]{:S(2)}) copy-start(f32[2,16,64,128]{3,2,1,0:T(8,128)} %get-tuple-element.329) | copy-start | bytes 3145732
  220.6 35.6 %all-to-all-start = ((f32[8,1,65536]{2,1,0:T(1,128)}), f32[8,1,65536]{2,1,0:T(1,128)}, u32[]{:S(2)}, u32[]{:S(2)}) async-start(f32[8,1,65536]{2,1,0:T(1,128)} %broadcast_in_dim.79), calls=%async_computation | async-start | bytes 4194304 | tf_op jit(solution)/shard_map/all_to_all | solution.py:41
  227.3 1.2 copy-start.8
  233.0 27.0 %copy-start.1 = (bf16[256,1024]{1,0:T(8,128)(2,1)S(1)}, bf16[256,1024]{1,0:T(8,128)(2,1)}, u32[]{:S(2)}) copy-start(bf16[256,1024]{1,0:T(8,128)(2,1)} %param.16) | copy-start | bytes 1572868
Sparse Core Ops, SparseCore 0:
  10.3 36.1 all-gather.6
  48.2 52.2 all-gather.8
  137.8 51.4 all-gather.10
where the time goes:
time: 270 us; the launch traced here: 267 us
  other arithmetic  66.3 us (25%)
  waiting for transfers between devices  58 us (21%)
  matrix products  54.1 us (20%)
  local copies, waits for them, and re-layouts  34.2 us (13%)
  blocking collectives  31.2 us (12%)
  between operations  14.7 us (5%)
  starting transfers between devices  6.82 us (3%)
    all_gather x2, waiting for transfers between devices, prefix(): pieces = jax.tree.map(lambda part: lax.all_gather(part, axis), value)  38.1 us
    select_n x30, other arithmetic, hop(): jnp.where(position < mine, new, old)  35.3 us
    unnamed x1, blocking collectives  31.2 us
    all_to_all x1, waiting for transfers between devices, sent_to_all(): lax.all_to_all(jnp.broadcast_to(array[None], (devices, *array.shape)), ax...  19.8 us
    dot_general x1, matrix products, teacher_attention(): jnp.einsum('grij,jgd->igrd', weights.astype(jnp.bfloat16), value_heads, p...  15.9 us
    reduce_sum x1, other arithmetic, teacher_attention(): new_sum = jnp.sum(weights, axis=-1)  15.5 us
    dot_general x1, matrix products, teacher_attention(): jnp.einsum('igrd,jgd->grij', grouped, key_heads, preferred_element_type=j...  15.4 us
    unnamed x39, local copies, waits for them, and re-layouts  12.4 us
  transfers between devices with their start and end apart: 4, of which 2 were waited for; matrix products, arithmetic and copies ran while one was open for 32% of the time, Pallas kernels for 0%

commit v1 on v0

v1 whole, which is shorter than its diff:
```python
import functools
import math

import jax
import jax.numpy as jnp
from jax import lax
from jax.experimental import pallas as pl
from jax.experimental.pallas import tpu as pltpu
from jax.sharding import PartitionSpec as P

MESH = pl.DeviceIdType.MESH
F32, BF16 = jnp.float32, jnp.bfloat16
TOK = 256
HD = 128
LOW = -1e30
SEQ = 16
CHIPS = 8
PAIRS = 8
TP = 8
SCALE = math.log2(math.e) / math.sqrt(HD)


def dot(a, b):
    return jnp.dot(a, b, preferred_element_type=F32)


def dot_nt(a, b):
    return lax.dot_general(a, b, (((1,), (1,)), ((), ())), preferred_element_type=F32)


def halves(a):
    high = a.astype(BF16)
    return high, (a - high.astype(F32)).astype(BF16)


def three(op, a, b):
    (ah, al), (bh, bl) = halves(a), halves(b)
    return op(ah, bh) + op(al, bh) + op(ah, bl)


def remote(src, dst, send_sem, recv_sem, axis, index):
    return pltpu.make_async_remote_copy(
        src_ref=src,
        dst_ref=dst,
        send_sem=send_sem,
        recv_sem=recv_sem,
        device_id={axis: index},
        device_id_type=MESH,
    )


def main_kernel(
    q_ref,
    k_ref,
    v_ref,
    x_ref,
    w_ref,
    r_ref,
    ls_ref,
    ld_ref,
    gi_ref,
    gwr_ref,
    gls_ref,
    keys,
    values,
    scores,
    peak,
    total,
    mixed,
    decay_buf,
    mix_high,
    mix_low,
    from_start,
    in_scale,
    local_y,
    back,
    wt_buf,
    rt_buf,
    pair_buf,
    lane_decay,
    fwd_local,
    fwd_sibling,
    fwd_chip,
    fwd_got,
    fwd_out,
    fwd_in,
    state_in,
    bwd_local,
    bwd_sibling,
    bwd_chip,
    bwd_got,
    bwd_out,
    bwd_in,
    key_send,
    key_recv,
    value_send,
    value_recv,
    sib_send,
    sib_recv,
    leg_send,
    leg_recv,
    ret_send,
    ret_recv,
):
    me = lax.axis_index("seq")
    core = lax.rem(me, 2)
    chip = me // 2
    sibling = me + 1 - 2 * core
    partner = me + 2 - 4 * lax.rem(chip, 2)
    above = lax.rem(me + 4, SEQ)
    below = lax.rem(me + 12, SEQ)
    far = lax.rem(me + 8, SEQ)
    above_p, below_p = lax.rem(partner + 4, SEQ), lax.rem(partner + 12, SEQ)
    far_p = lax.rem(partner + 8, SEQ)
    started = []

    barrier = pltpu.get_barrier_semaphore()
    for hop in range(1, SEQ):
        pl.semaphore_signal(
            barrier,
            inc=1,
            device_id={"seq": lax.rem(me + hop, SEQ)},
            device_id_type=MESH,
        )

    log_decay = ld_ref[...]
    log_step = ls_ref[...]
    rows = lax.broadcasted_iota(jnp.int32, (TOK, TOK), 0)
    cols = lax.broadcasted_iota(jnp.int32, (TOK, TOK), 1)
    causal = rows >= cols
    upper = jnp.where(rows <= cols, 1.0, 0.0).astype(BF16)
    d1 = log_decay.astype(BF16)
    rest = log_decay - d1.astype(F32)
    d2 = rest.astype(BF16)
    d3 = (rest - d2.astype(F32)).astype(BF16)
    cum = dot(d1, upper) + dot(d2, upper) + dot(d3, upper)
    end = cum[:, TOK - 1 : TOK]
    row_term = log_step - cum
    log_in = row_term + end
    columns = jnp.concatenate([cum, log_in, jnp.zeros((96, TOK), F32)], axis=0).T
    lane = lax.broadcasted_iota(jnp.int32, (TOK, HD), 1)
    first = lane < 64
    lane8 = lax.broadcasted_iota(jnp.int32, (8, HD), 1)
    wt_buf[...] = w_ref[...].T
    rt_buf[...] = r_ref[...].T
    for t in range(PAIRS):
        a, b = 2 * t, 2 * t + 1
        at = slice(t * HD, (t + 1) * HD)
        from_start[:, at] = jnp.exp(
            jnp.where(first, columns[:, a : a + 1], columns[:, b : b + 1])
        )
        scale = jnp.exp(
            jnp.where(first, columns[:, 16 + a : 17 + a], columns[:, 16 + b : 17 + b])
        )
        in_scale[:, at] = scale
        tile = jnp.where(lane8 < 64, end[a : a + 1, :], end[b : b + 1, :])
        lane_decay[t] = tile
        high, low = halves(x_ref[:, at].astype(F32) * scale)
        state = dot(wt_buf[...], high) + dot(wt_buf[...], low)
        for half in range(2):
            fwd_local[t, half, 0:64] = state[half * 64 : (half + 1) * 64]
            fwd_local[t, half, 64:72] = tile

    pl.semaphore_wait(barrier, SEQ - 1)

    def begin(copy):
        copy.start()
        started.append(copy)

    count = [0]

    def pass_block(source, index, target):
        n = count[0]
        count[0] += 1
        src_k = k_ref if source is None else keys.at[index]
        src_v = v_ref if source is None else values.at[index]
        begin(remote(src_k, keys.at[index], key_send.at[n], key_recv.at[index], "seq", target))
        begin(
            remote(src_v, values.at[index], value_send.at[n], value_recv.at[index], "seq", target)
        )

    def await_block(index):
        remote(
            keys.at[index], keys.at[index], key_send.at[0], key_recv.at[index], "seq", sibling
        ).wait_recv()
        remote(
            values.at[index], values.at[index], value_send.at[0], value_recv.at[index], "seq", sibling
        ).wait_recv()

    for target in (partner, above, below, sibling):
        pass_block(None, me, target)
    begin(remote(fwd_local, fwd_sibling, sib_send.at[0], sib_recv.at[0], "seq", sibling))
    keys[me] = k_ref[...]
    values[me] = v_ref[...]

    inner = dot_nt(r_ref[...], w_ref[...])

    def build(h):
        gap = columns[:, h : h + 1] + row_term[h : h + 1, :]
        decay = jnp.where(causal, jnp.exp(gap), 0.0)
        decay_buf[h] = decay
        high, low = halves(decay * inner)
        mix_high[h] = high
        mix_low[h] = low

    for h in range(8):
        build(h)

    def chip_states(local, sib, out, early_first):
        for t in range(PAIRS):
            mine, other = local[t, core], sib[t, core]
            early = jnp.where(core == 0, mine, other)
            late = jnp.where(core == 0, other, mine)
            if not early_first:
                early, late = late, early
            out[t, 0:64] = early[0:64] * jnp.exp(late[64:65]) + late[0:64]
            out[t, 64:72] = early[64:72] + late[64:72]

    def send_leg(stage, chip_buf, got):
        got[chip] = chip_buf[chip]
        for hop in range(1, CHIPS):
            target = lax.rem(chip + hop, CHIPS)
            begin(
                remote(
                    chip_buf.at[target],
                    got.at[chip],
                    leg_send.at[stage, hop],
                    leg_recv.at[stage, chip],
                    "seq",
                    2 * target + core,
                )
            )

    def scan_leg(stage, got, out, into, order):
        for hop in range(1, CHIPS):
            source = lax.rem(chip + hop, CHIPS)
            remote(
                got.at[source],
                got.at[source],
                leg_send.at[stage, 0],
                leg_recv.at[stage, source],
                "seq",
                sibling,
            ).wait_recv()
        running = jnp.zeros((64, HD), F32)
        for i in order:
            out[i] = running
            running = running * jnp.exp(got[i, 64:65]) + got[i, 0:64]
        into[core, chip] = out[chip]
        for hop in range(1, CHIPS):
            target = lax.rem(chip + hop, CHIPS)
            begin(
                remote(
                    out.at[target],
                    into.at[core, chip],
                    ret_send.at[stage, hop],
                    ret_recv.at[stage, chip],
                    "seq",
                    2 * target + core,
                )
            )

    def spread(stage, into):
        for hop in range(1, CHIPS):
            source = lax.rem(chip + hop, CHIPS)
            remote(
                into.at[core, source],
                into.at[core, source],
                ret_send.at[stage, 0],
                ret_recv.at[stage, source],
                "seq",
                sibling,
            ).wait_recv()
        begin(
            remote(
                into.at[core],
                into.at[core],
                sib_send.at[2 * stage + 1],
                sib_recv.at[2 * stage + 1],
                "seq",
                sibling,
            )
        )
        remote(
            into.at[1 - core],
            into.at[1 - core],
            sib_send.at[2 * stage + 1],
            sib_recv.at[2 * stage + 1],
            "seq",
            sibling,
        ).wait_recv()

    remote(
        fwd_sibling, fwd_sibling, sib_send.at[0], sib_recv.at[0], "seq", sibling
    ).wait_recv()
    chip_states(fwd_local, fwd_sibling, fwd_chip, True)
    send_leg(0, fwd_chip, fwd_got)

    await_block(partner)
    for target in (above, below, sibling):
        pass_block(keys, partner, target)

    for h in range(8, 16):
        build(h)

    await_block(below)
    for target in (above, sibling):
        pass_block(keys, below, target)
    await_block(above_p)
    for target in (below, sibling):
        pass_block(keys, above_p, target)

    scan_leg(0, fwd_got, fwd_out, fwd_in, range(CHIPS))

    def make_y(t, carry):
        at = pl.ds(pl.multiple_of(t * HD, HD), HD)
        x = x_ref[:, at]
        xa = jnp.where(first, x, jnp.zeros_like(x))
        xb = jnp.where(first, jnp.zeros_like(x), x)
        local_y[:, at] = (
            dot(mix_high[2 * t], xa)
            + dot(mix_low[2 * t], xa)
            + dot(mix_high[2 * t + 1], xb)
            + dot(mix_low[2 * t + 1], xb)
        )
        return carry

    lax.fori_loop(0, PAIRS, make_y, 0)

    for index in (above, below_p, far, far_p):
        await_block(index)
        pass_block(keys, index, sibling)
    for index in (me, partner, above, below, above_p, below_p, far, far_p):
        await_block(index + 1 - 2 * core)

    peak[...] = jnp.full(peak.shape, LOW, F32)

    def score_block(b, mask):
        kt = keys[b].T
        for h in range(8):
            at = slice(h * TOK, (h + 1) * TOK)
            s = dot(q_ref[:, h * HD : (h + 1) * HD], kt)
            if mask:
                s = jnp.where(causal, s, LOW)
            scores[b, at] = s
            peak[at] = jnp.maximum(peak[at], jnp.maximum(s[:, :HD], s[:, HD:]))

    def score_step(b, carry):
        score_block(b, False)
        return carry

    lax.fori_loop(0, me, score_step, 0)
    score_block(me, True)

    @pl.when(core == 0)
    def _():
        scores[me + 1] = jnp.full((8 * TOK, TOK), LOW, F32)

    spread(0, fwd_in)
    pair_buf[...] = jnp.zeros(pair_buf.shape, F32)
    gwr_ref[...] = jnp.zeros(gwr_ref.shape, F32)

    def group(g, carry):
        at2 = pl.ds(pl.multiple_of(g * 2 * TOK, 2 * TOK), 2 * TOK)
        top = jnp.max(peak[at2], axis=1, keepdims=True) * SCALE
        total[...] = jnp.zeros(total.shape, F32)
        mixed[...] = jnp.zeros(mixed.shape, F32)

        def chunk(n, inner_carry):
            for b in (2 * n, 2 * n + 1):
                weights = jnp.exp2(scores[b, at2] * SCALE - top)
                total[...] += weights[:, :HD] + weights[:, HD:]
                mixed[...] += dot(weights.astype(BF16), values[b])
            return inner_carry

        lax.fori_loop(0, chip + 1, chunk, 0)
        ratio = mixed[...] / jnp.sum(total[...], axis=1, keepdims=True)
        taught = ratio.astype(BF16).astype(F32)
        for part in range(2):
            t = 2 * g + part
            at = pl.ds(pl.multiple_of(t * HD, HD), HD)
            entering = jnp.concatenate([fwd_in[0, t], fwd_in[1, t]], axis=0)
            sib = fwd_sibling[t]
            sib_state = jnp.concatenate([sib[0, 0:64], sib[1, 0:64]], axis=0)
            entering = jnp.where(
                core == 1, entering * jnp.exp(sib[0, 64:65]) + sib_state, entering
            )
            state_in[t] = entering
            sh, sl = halves(entering)
            starts = from_start[:, at]
            carried = (dot(r_ref[...], sh) + dot(r_ref[...], sl)) * starts
            residual = local_y[:, at] + carried - taught[part * TOK : (part + 1) * TOK]
            local_y[:, at] = residual
            wh, wl = halves(residual * starts)
            adjoint = dot(rt_buf[...], wh) + dot(rt_buf[...], wl)
            for half in range(2):
                bwd_local[t, half, 0:64] = adjoint[half * 64 : (half + 1) * 64]
                bwd_local[t, half, 64:72] = lane_decay[t]
        return carry

    lax.fori_loop(0, PAIRS // 2, group, 0)

    begin(remote(bwd_local, bwd_sibling, sib_send.at[2], sib_recv.at[2], "seq", sibling))
    remote(
        bwd_sibling, bwd_sibling, sib_send.at[2], sib_recv.at[2], "seq", sibling
    ).wait_recv()
    chip_states(bwd_local, bwd_sibling, bwd_chip, False)
    send_leg(1, bwd_chip, bwd_got)

    def local_terms(t, carry):
        at = pl.ds(pl.multiple_of(t * HD, HD), HD)
        residual = local_y[:, at]
        xt = x_ref[:, at].T
        for part, own in ((0, first), (1, ~first)):
            rh, rl = halves(jnp.where(own, residual, 0.0))
            pair_buf[...] += decay_buf[2 * t + part] * (dot(rh, xt) + dot(rl, xt))
        return carry

    def back_terms(t, carry):
        at = pl.ds(pl.multiple_of(t * HD, HD), HD)
        residual_t = local_y[:, at].T
        rh, rl = halves(residual_t)
        pieces = []
        for part in range(2):
            own = slice(part * 64, (part + 1) * 64)
            both = jnp.concatenate([rh[own], rl[own]], axis=0)
            product = dot(both, mix_high[2 * t + part])
            pieces.append(product[0:64] + product[64:128] + dot(rh[own], mix_low[2 * t + part]))
        back[:, at] = jnp.concatenate(pieces, axis=0).T
        return carry

    def read_terms(t, carry):
        at = pl.ds(pl.multiple_of(t * HD, HD), HD)
        weighted = local_y[:, at] * from_start[:, at]
        gwr_ref[TOK : 2 * TOK] += three(dot_nt, weighted, state_in[t])
        return carry

    lax.fori_loop(0, PAIRS, local_terms, 0)
    scan_leg(1, bwd_got, bwd_out, bwd_in, range(CHIPS - 1, -1, -1))
    lax.fori_loop(0, PAIRS, back_terms, 0)
    lax.fori_loop(0, PAIRS, read_terms, 0)
    ph, pl_ = halves(pair_buf[...])
    gwr_ref[TOK : 2 * TOK] += dot(ph, w_ref[...]) + dot(pl_, w_ref[...])
    th, tl = halves(pair_buf[...].T)
    gwr_ref[0:TOK] += dot(th, r_ref[...]) + dot(tl, r_ref[...])
    spread(1, bwd_in)

    row8 = lax.broadcasted_iota(jnp.int32, (8, HD), 0)
    pick = jnp.where((lane8 < 64) == (row8 == 0), 1.0, 0.0)
    pick = jnp.where(row8 < 2, pick, 0.0).astype(BF16)

    def finish(t, carry):
        at = pl.ds(pl.multiple_of(t * HD, HD), HD)
        arriving = jnp.concatenate([bwd_in[0, t], bwd_in[1, t]], axis=0)
        sib = bwd_sibling[t]
        sib_state = jnp.concatenate([sib[0, 0:64], sib[1, 0:64]], axis=0)
        arriving = jnp.where(
            core == 0, arriving * jnp.exp(sib[0, 64:65]) + sib_state, arriving
        )
        ah, al = halves(arriving)
        x = x_ref[:, at].astype(F32)
        scale = in_scale[:, at]
        grad = back[:, at] + scale * (dot(w_ref[...], ah) + dot(w_ref[...], al))
        gi_ref[:, at] = grad
        gh, gl = halves(x * grad)
        sums = dot_nt(pick, gh) + dot_nt(pick, gl)
        gls_ref[t] = sums[0:2]
        gwr_ref[0:TOK] += three(dot_nt, x * scale, arriving)
        return carry

    lax.fori_loop(0, PAIRS, finish, 0)

    for copy in started:
        copy.wait_send()


def reduce_kernel(g_ref, gw_ref, gr_ref, got, part, whole, send, recv, send2, recv2):
    me = lax.axis_index("tp")
    depth = 2 * TOK // TP
    barrier = pltpu.get_barrier_semaphore()
    for hop in range(1, TP):
        pl.semaphore_signal(
            barrier, inc=1, device_id={"tp": lax.rem(me + hop, TP)}, device_id_type=MESH
        )
    pl.semaphore_wait(barrier, TP - 1)
    copies = []
    for hop in range(1, TP):
        to = lax.rem(me + hop, TP)
        copies.append(
            remote(
                g_ref.at[pl.ds(pl.multiple_of(to * depth, depth), depth)],
                got.at[me],
                send.at[hop],
                recv.at[me],
                "tp",
                to,
            )
        )
        copies[-1].start()
    got[me] = g_ref[pl.ds(pl.multiple_of(me * depth, depth), depth)]
    for hop in range(1, TP):
        source = lax.rem(me + hop, TP)
        remote(got.at[source], got.at[source], send.at[0], recv.at[source], "tp", source).wait_recv()
    acc = got[0]
    for i in range(1, TP):
        acc = acc + got[i]
    part[...] = acc
    for hop in range(1, TP):
        to = lax.rem(me + hop, TP)
        copies.append(
            remote(part, whole.at[me], send2.at[hop], recv2.at[me], "tp", to)
        )
        copies[-1].start()
    whole[me] = acc
    for hop in range(1, TP):
        source = lax.rem(me + hop, TP)
        remote(
            whole.at[source], whole.at[source], send2.at[0], recv2.at[source], "tp", source
        ).wait_recv()
    for i in range(TP // 2):
        gw_ref[i * depth : (i + 1) * depth] = whole[i]
        gr_ref[i * depth : (i + 1) * depth] = whole[TP // 2 + i]
    for copy in copies:
        copy.wait_send()


def vmem():
    return pl.BlockSpec(memory_space=pltpu.VMEM)


def on_device(
    query_rows, key_rows, value_rows, mixer_input, write_rows, read_rows, log_step, log_decay
):
    dma = pltpu.SemaphoreType.DMA
    packet = (PAIRS, 2, 72, HD)
    exchange = [
        pltpu.VMEM(packet, F32),
        pltpu.VMEM(packet, F32),
        pltpu.VMEM((PAIRS, 72, HD), F32),
        pltpu.VMEM((CHIPS, 72, HD), F32),
        pltpu.VMEM((CHIPS, 64, HD), F32),
        pltpu.VMEM((2, PAIRS, 64, HD), F32),
    ]
    grad_input, sums, grad_step = pl.pallas_call(
        main_kernel,
        out_shape=(
            jax.ShapeDtypeStruct((TOK, PAIRS * HD), F32),
            jax.ShapeDtypeStruct((2 * TOK, HD), F32),
            jax.ShapeDtypeStruct((PAIRS, 2, TOK), F32),
        ),
        in_specs=[vmem()] * 8,
        out_specs=(vmem(),) * 3,
        scratch_shapes=[
            pltpu.VMEM((SEQ, TOK, HD), BF16),
            pltpu.VMEM((SEQ, TOK, HD), BF16),
            pltpu.VMEM((SEQ, 8 * TOK, TOK), F32),
            pltpu.VMEM((8 * TOK, HD), F32),
            pltpu.VMEM((2 * TOK, HD), F32),
            pltpu.VMEM((2 * TOK, HD), F32),
            pltpu.VMEM((16, TOK, TOK), F32),
            pltpu.VMEM((16, TOK, TOK), BF16),
            pltpu.VMEM((16, TOK, TOK), BF16),
            pltpu.VMEM((TOK, PAIRS * HD), F32),
            pltpu.VMEM((TOK, PAIRS * HD), F32),
            pltpu.VMEM((TOK, PAIRS * HD), F32),
            pltpu.VMEM((TOK, PAIRS * HD), F32),
            pltpu.VMEM((HD, TOK), BF16),
            pltpu.VMEM((HD, TOK), BF16),
            pltpu.VMEM((TOK, TOK), F32),
            pltpu.VMEM((PAIRS, 8, HD), F32),
            *exchange,
            pltpu.VMEM((PAIRS, HD, HD), F32),
            *exchange,
            dma((16,)),
            dma((SEQ,)),
            dma((16,)),
            dma((SEQ,)),
            dma((4,)),
            dma((4,)),
            dma((2, CHIPS)),
            dma((2, CHIPS)),
            dma((2, CHIPS)),
            dma((2, CHIPS)),
        ],
        compiler_params=pltpu.CompilerParams(
            collective_id=0, has_side_effects=True, vmem_limit_bytes=60 * 1024 * 1024
        ),
        name="distill",
    )(query_rows, key_rows, value_rows, mixer_input, write_rows, read_rows, log_step, log_decay)
    depth = 2 * TOK // TP
    grad_write, grad_read = pl.pallas_call(
        reduce_kernel,
        out_shape=(jax.ShapeDtypeStruct((TOK, HD), F32),) * 2,
        in_specs=[vmem()],
        out_specs=(vmem(),) * 2,
        scratch_shapes=[
            pltpu.VMEM((TP, depth, HD), F32),
            pltpu.VMEM((depth, HD), F32),
            pltpu.VMEM((TP, depth, HD), F32),
            dma((TP,)),
            dma((TP,)),
            dma((TP,)),
            dma((TP,)),
        ],
        compiler_params=pltpu.CompilerParams(collective_id=1, has_side_effects=True),
        name="share",
    )(sums)
    return grad_input, grad_write, grad_read, grad_step.reshape(2 * PAIRS, TOK)


def solution(mesh):
    in_specs = (
        P("seq", "tp"),
        P("seq", "tp"),
        P("seq", "tp"),
        P("seq", "tp"),
        P("seq", None),
        P("seq", None),
        P("tp", "seq"),
        P("tp", "seq"),
    )
    out_specs = (P("seq", "tp"), P("seq", None), P("seq", None), P("tp", "seq"))
    return jax.shard_map(
        on_device, mesh=mesh, in_specs=in_specs, out_specs=out_specs, check_vma=False
    )
```

time: 270 us -> 89.4 us (0.33); the launches traced: 267 us -> 89.1 us
  Pallas kernels: 0 us -> 83.2 us
  other arithmetic: 66.3 us -> 0 us
  waiting for transfers between devices: 58 us -> 0 us
  matrix products: 54.1 us -> 0 us
  blocking collectives: 31.2 us -> 0 us
  local copies, waits for them, and re-layouts: 34.2 us -> 5.29 us
  between operations: 14.7 us -> 0.66 us
  starting transfers between devices: 6.82 us -> 0 us
    pallas_call x0 -> x2, Pallas kernels: none -> 83.2 us  [the longest x1 63.8 us: on_device(): pl.pallas_call(main_kernel, out_shape=(jax.ShapeDtypeStruct((TOK, PAIRS *...]
    dot_general x14 -> x0, matrix products: 54.1 us -> none  [the longest x1 15.9 us: teacher_attention(): jnp.einsum('grij,jgd->igrd', weights.astype(jnp.bfloat16), value_heads, p...]
    all_gather x3 -> x0, waiting for transfers between devices: 38.1 us -> none  [the longest x2 38.1 us: prefix(): pieces = jax.tree.map(lambda part: lax.all_gather(part, axis), value)]
    select_n x30 -> x0, other arithmetic: 35.3 us -> none  [hop(): jnp.where(position < mine, new, old)]
    unnamed x1 -> x0, blocking collectives: 31.2 us -> none
    all_to_all x1 -> x0, waiting for transfers between devices: 19.8 us -> none  [sent_to_all(): lax.all_to_all(jnp.broadcast_to(array[None], (devices, *array.shape)), ax...]
    reduce_sum x3 -> x0, other arithmetic: 18.8 us -> none  [the longest x1 15.5 us: teacher_attention(): new_sum = jnp.sum(weights, axis=-1)]
    unnamed x39 -> x7, local copies, waits for them, and re-layouts: 12.4 us -> 3.95 us
  transfers between devices with their start and end apart: 4 -> 0, of which waited for: 2 -> 0; matrix products, arithmetic and copies ran while one was open for 32% -> 0% of each run, Pallas kernels for 0% -> 0%
where the time goes in v1:
time: 89.4 us; the launch traced here: 89.1 us
  Pallas kernels  83.2 us (93%)
  local copies, waits for them, and re-layouts  5.29 us (6%)
    pallas_call x1, Pallas kernels, on_device(): pl.pallas_call(main_kernel, out_shape=(jax.ShapeDtypeStruct((TOK, PAIRS *...  63.8 us
    pallas_call x1, Pallas kernels, on_device(): pl.pallas_call(reduce_kernel, out_shape=(jax.ShapeDtypeStruct((TOK, HD),...  19.4 us
    unnamed x7, local copies, waits for them, and re-layouts  3.95 us

profile of v1, /device:TPU:0, one launch (start us, length us, event | category | flops | bytes accessed | tf_op | source)
XLA Modules:
  0.0 89.1 jit_solution(14084787661983433919)
XLA Ops:
  0.6 63.8 %distill.1 = (f32[256,1024]{1,0:T(8,128)}, f32[512,128]{1,0:T(8,128)}, f32[8,2,256]{2,1,0:T(2,128)}) custom-call(bf16[256,1024]{1,0:T(8,128)(2,1)} %q_ref.1, bf16[256,128]{1,0:T(8,128)(2,1)} %k_ref.1, bf16[256,128]{1,0:T(8,128)(2,1)} %v_ref.1, bf16[256,1024]{1,0:T(8,128)(2,1)} %x_ref.1, bf16[256,128]{1,0:T(8,128)(2,1)} %w_ref.1, bf16[256,128]{1,0:T(8,128)(2,1)} %r_ref.1, ...), custom_call_target="tpu_custom_call" | custom-call | tf_op jit(solution)/shard_map/distill/pallas_call | solution.py:544
  64.4 1.3 %reshape.11 = f32[16,256]{1,0:T(8,128)} reshape(f32[8,2,256]{2,1,0:T(2,128)} %get-tuple-element.13) | data formatting | bytes 32768 | tf_op jit(solution)/shard_map/reshape | solution.py:608
  65.8 19.4 %share.1 = (f32[256,128]{1,0:T(8,128)}, f32[256,128]{1,0:T(8,128)}) custom-call(f32[512,128]{1,0:T(8,128)} %get-tuple-element.10.g_ref), custom_call_target="tpu_custom_call" | custom-call | tf_op jit(solution)/shard_map/share/pallas_call | solution.py:591
  85.2 0.0 copy-start.1
  85.2 2.3 %copy.15 = f32[256,1024]{1,0:T(8,128)} copy(f32[256,1024]{1,0:T(8,128)} %get-tuple-element.18) | data formatting | bytes 2097152
  87.5 0.0 copy-done.1
  87.5 0.0 copy-start
  87.5 0.7 copy.16
  88.2 0.3 copy-done
  88.5 0.7 copy.17
Async XLA Ops:
  85.2 2.4 %copy-start.1 = (f32[256,128]{1,0:T(8,128)S(1)}, f32[256,128]{1,0:T(8,128)}, u32[]{:S(2)}) copy-start(f32[256,128]{1,0:T(8,128)} %get-tuple-element.19) | copy-start | bytes 393220
  87.5 1.0 %copy-start = (f32[256,128]{1,0:T(8,128)S(1)}, f32[256,128]{1,0:T(8,128)}, u32[]{:S(2)}) copy-start(f32[256,128]{1,0:T(8,128)} %get-tuple-element.20) | copy-start | bytes 393220

commit v2 on v1

v2 whole, which is shorter than its diff:
```python
import functools
import math

import jax
import jax.numpy as jnp
from jax import lax
from jax.experimental import pallas as pl
from jax.experimental.pallas import tpu as pltpu
from jax.sharding import PartitionSpec as P

MESH = pl.DeviceIdType.MESH
F32, BF16 = jnp.float32, jnp.bfloat16
TOK = 256
HD = 128
LOW = -1e30
SEQ = 16
CHIPS = 8
PAIRS = 8
TP = 8
SCALE = math.log2(math.e) / math.sqrt(HD)


def dot(a, b):
    return jnp.dot(a, b, preferred_element_type=F32)


def dot_nt(a, b):
    return lax.dot_general(a, b, (((1,), (1,)), ((), ())), preferred_element_type=F32)


def halves(a):
    high = a.astype(BF16)
    return high, (a - high.astype(F32)).astype(BF16)


def three(op, a, b):
    (ah, al), (bh, bl) = halves(a), halves(b)
    return op(ah, bh) + op(al, bh) + op(ah, bl)


def remote(src, dst, send_sem, recv_sem, axis, index):
    return pltpu.make_async_remote_copy(
        src_ref=src,
        dst_ref=dst,
        send_sem=send_sem,
        recv_sem=recv_sem,
        device_id={axis: index},
        device_id_type=MESH,
    )


def main_kernel(
    q_hbm,
    k_hbm,
    v_hbm,
    x_hbm,
    w_hbm,
    r_hbm,
    ls_hbm,
    ld_hbm,
    gi_hbm,
    gw_ref,
    gr_ref,
    gls_ref,
    q_ref,
    x_ref,
    w_ref,
    r_ref,
    ls_ref,
    ld_ref,
    keys,
    values,
    scores,
    peak,
    total,
    mixed,
    taught,
    decay_buf,
    mix_high,
    mix_low,
    from_start,
    in_scale,
    local_y,
    back,
    wt_buf,
    rt_buf,
    pair_buf,
    sums,
    lane_decay,
    fwd_local,
    fwd_sibling,
    fwd_chip,
    fwd_got,
    fwd_out,
    fwd_in,
    state_in,
    bwd_local,
    bwd_sibling,
    bwd_chip,
    bwd_got,
    bwd_out,
    bwd_in,
    early,
    early_got,
    part,
    read_all,
    late,
    late_got,
    write_part,
    write_all,
    in_sem,
    out_sem,
    key_send,
    key_recv,
    value_send,
    value_recv,
    sib_send,
    sib_recv,
    leg_send,
    leg_recv,
    ret_send,
    ret_recv,
    tp_send,
    tp_recv,
):
    me = lax.axis_index("seq")
    tp = lax.axis_index("tp")
    core = lax.rem(me, 2)
    chip = me // 2
    plane = lax.rem(chip, 2)
    row = me // 4
    sibling = me + 1 - 2 * core
    partner = me + 2 - 4 * plane
    above = lax.rem(me + 4, SEQ)
    below = lax.rem(me + 12, SEQ)
    far = lax.rem(me + 8, SEQ)
    above_p, below_p = lax.rem(partner + 4, SEQ), lax.rem(partner + 12, SEQ)
    far_p = lax.rem(partner + 8, SEQ)
    started = []

    barrier = pltpu.get_barrier_semaphore()
    for hop in range(1, SEQ):
        pl.semaphore_signal(
            barrier,
            inc=1,
            device_id={"seq": lax.rem(me + hop, SEQ)},
            device_id_type=MESH,
        )
    for hop in range(1, TP):
        pl.semaphore_signal(
            barrier,
            inc=1,
            device_id={"tp": lax.rem(tp + hop, TP)},
            device_id_type=MESH,
        )
    loads = [
        pltpu.make_async_copy(src, dst, in_sem.at[n])
        for n, (src, dst) in enumerate(
            (
                (k_hbm, keys.at[me]),
                (v_hbm, values.at[me]),
                (ld_hbm, ld_ref),
                (ls_hbm, ls_ref),
                (w_hbm, w_ref),
                (x_hbm, x_ref),
                (r_hbm, r_ref),
                (q_hbm, q_ref),
            )
        )
    ]
    for load in loads:
        load.start()

    def begin(copy):
        copy.start()
        started.append(copy)

    count = [0, 0]

    def pass_on(kind, index, *targets):
        store, send, recv = ((keys, key_send, key_recv), (values, value_send, value_recv))[kind]
        for target in targets:
            n = count[kind]
            count[kind] += 1
            begin(remote(store.at[index], store.at[index], send.at[n], recv.at[index], "seq", target))

    def arrived(kind, index):
        store, send, recv = ((keys, key_send, key_recv), (values, value_send, value_recv))[kind]
        remote(
            store.at[index], store.at[index], send.at[0], recv.at[index], "seq", sibling
        ).wait_recv()

    loads[0].wait()
    loads[1].wait()
    pl.semaphore_wait(barrier, SEQ + TP - 2)
    for kind in range(2):
        pass_on(kind, me, partner, above, below, sibling)

    def relay_one(kind):
        arrived(kind, partner)
        pass_on(kind, partner, above, below, sibling)
        arrived(kind, below)
        pass_on(kind, below, above, sibling)

    def relay_two(kind):
        arrived(kind, above_p)
        pass_on(kind, above_p, below, sibling)
        for index in (above, below_p):
            arrived(kind, index)
            pass_on(kind, index, sibling)

    def relay_three(kind):
        for index in (far, far_p):
            arrived(kind, index)
            pass_on(kind, index, sibling)

    rows = lax.broadcasted_iota(jnp.int32, (TOK, TOK), 0)
    cols = lax.broadcasted_iota(jnp.int32, (TOK, TOK), 1)
    causal = rows >= cols
    upper = jnp.where(rows <= cols, 1.0, 0.0).astype(BF16)
    for load in loads[2:6]:
        load.wait()
    log_decay = ld_ref[...]
    d1 = log_decay.astype(BF16)
    rest = log_decay - d1.astype(F32)
    d2 = rest.astype(BF16)
    d3 = (rest - d2.astype(F32)).astype(BF16)
    cum = dot(d1, upper) + dot(d2, upper) + dot(d3, upper)
    end = cum[:, TOK - 1 : TOK]
    row_term = ls_ref[...] - cum
    log_in = row_term + end
    columns = jnp.concatenate([cum, log_in, jnp.zeros((96, TOK), F32)], axis=0).T
    lane = lax.broadcasted_iota(jnp.int32, (TOK, HD), 1)
    first = lane < 64
    lane8 = lax.broadcasted_iota(jnp.int32, (8, HD), 1)
    wt_buf[...] = w_ref[...].T
    for t in range(PAIRS):
        a, b = 2 * t, 2 * t + 1
        at = slice(t * HD, (t + 1) * HD)
        from_start[:, at] = jnp.exp(
            jnp.where(first, columns[:, a : a + 1], columns[:, b : b + 1])
        )
        scale = jnp.exp(
            jnp.where(first, columns[:, 16 + a : 17 + a], columns[:, 16 + b : 17 + b])
        )
        in_scale[:, at] = scale
        tile = jnp.where(lane8 < 64, end[a : a + 1, :], end[b : b + 1, :])
        lane_decay[t] = tile
        high, low = halves(x_ref[:, at].astype(F32) * scale)
        state = dot(wt_buf[...], high) + dot(wt_buf[...], low)
        for half in range(2):
            fwd_local[t, half, 0:64] = state[half * 64 : (half + 1) * 64]
            fwd_local[t, half, 64:72] = tile
    begin(remote(fwd_local, fwd_sibling, sib_send.at[0], sib_recv.at[0], "seq", sibling))
    loads[6].wait()
    rt_buf[...] = r_ref[...].T
    inner = dot_nt(r_ref[...], w_ref[...])
    relay_one(0)

    def build(h):
        gap = columns[:, h : h + 1] + row_term[h : h + 1, :]
        decay = jnp.where(causal, jnp.exp(gap), 0.0)
        decay_buf[h] = decay
        high, low = halves(decay * inner)
        mix_high[h] = high
        mix_low[h] = low

    def chip_state(t, local, sib, out, early_first):
        mine, other = local[t, core], sib[t, core]
        early_core = jnp.where(core == 0, mine, other)
        late_core = jnp.where(core == 0, other, mine)
        if not early_first:
            early_core, late_core = late_core, early_core
        out[t, 0:64] = early_core[0:64] * jnp.exp(late_core[64:65]) + late_core[0:64]
        out[t, 64:72] = early_core[64:72] + late_core[64:72]

    def leg(stage, t, chip_buf, got):
        return remote(
            chip_buf.at[t],
            got.at[chip],
            leg_send.at[stage, t],
            leg_recv.at[stage, chip],
            "seq",
            2 * t + core,
        )

    def send_leg(stage, t, chip_buf, got):
        @pl.when(chip != t)
        def _():
            leg(stage, t, chip_buf, got).start()

        @pl.when(chip == t)
        def _():
            got[t] = chip_buf[t]

    def scan_leg(stage, got, out, into, order):
        for hop in range(1, CHIPS):
            source = lax.rem(chip + hop, CHIPS)
            remote(
                got.at[source],
                got.at[source],
                leg_send.at[stage, 0],
                leg_recv.at[stage, source],
                "seq",
                sibling,
            ).wait_recv()
        running = jnp.zeros((64, HD), F32)
        for i in order:
            out[i] = running
            running = running * jnp.exp(got[i, 64:65]) + got[i, 0:64]
        into[core, chip] = out[chip]
        for hop in range(1, CHIPS):
            target = lax.rem(chip + hop, CHIPS)
            begin(
                remote(
                    out.at[target],
                    into.at[core, chip],
                    ret_send.at[stage, hop],
                    ret_recv.at[stage, chip],
                    "seq",
                    2 * target + core,
                )
            )

    def spread(stage, into):
        for hop in range(1, CHIPS):
            source = lax.rem(chip + hop, CHIPS)
            remote(
                into.at[core, source],
                into.at[core, source],
                ret_send.at[stage, 0],
                ret_recv.at[stage, source],
                "seq",
                sibling,
            ).wait_recv()
        begin(
            remote(
                into.at[core],
                into.at[core],
                sib_send.at[1 + stage],
                sib_recv.at[1 + stage],
                "seq",
                sibling,
            )
        )

    def spread_wait(stage, into):
        remote(
            into.at[1 - core],
            into.at[1 - core],
            sib_send.at[1 + stage],
            sib_recv.at[1 + stage],
            "seq",
            sibling,
        ).wait_recv()

    for h in range(8):
        build(h)
    relay_one(1)
    relay_two(0)

    loads[7].wait()
    peak[...] = jnp.full(peak.shape, LOW, F32)

    def score_block(b, mask):
        kt = keys[b].T
        for h in range(8):
            at = slice(h * TOK, (h + 1) * TOK)
            s = dot(q_ref[:, h * HD : (h + 1) * HD], kt) * SCALE
            if mask:
                s = jnp.where(causal, s, LOW)
            scores[b, at] = s
            peak[at] = jnp.maximum(peak[at], jnp.maximum(s[:, :HD], s[:, HD:]))

    def score_row(shift, low):
        def step(i, carry):
            flip = lax.rem(i, 2)
            b = (
                lax.rem(row + shift, 4) * 4
                + lax.rem(plane + i // 2, 2) * 2
                + lax.rem(core + flip, 2)
            )

            @pl.when(flip == 1)
            def _():
                arrived(0, b)

            @pl.when(b < me)
            def _():
                score_block(b, False)

            return carry

        lax.fori_loop(low, 4, step, 0)

    score_block(me, True)

    @pl.when(core == 0)
    def _():
        scores[me + 1] = jnp.full((8 * TOK, TOK), LOW, F32)

    for h in range(8, 16):
        build(h)
    score_row(0, 1)
    relay_two(1)
    relay_three(0)
    remote(
        fwd_sibling, fwd_sibling, sib_send.at[0], sib_recv.at[0], "seq", sibling
    ).wait_recv()
    for t in range(PAIRS):
        chip_state(t, fwd_local, fwd_sibling, fwd_chip, True)
        send_leg(0, t, fwd_chip, fwd_got)
    score_row(3, 0)
    score_row(1, 0)
    relay_three(1)

    def make_y(t, carry):
        at = pl.ds(pl.multiple_of(t * HD, HD), HD)
        x = x_ref[:, at]
        xa = jnp.where(first, x, jnp.zeros_like(x))
        xb = jnp.where(first, jnp.zeros_like(x), x)
        local_y[:, at] = (
            dot(mix_high[2 * t], xa)
            + dot(mix_low[2 * t], xa)
            + dot(mix_high[2 * t + 1], xb)
            + dot(mix_low[2 * t + 1], xb)
        )
        return carry

    lax.fori_loop(0, PAIRS, make_y, 0)
    score_row(2, 0)
    scan_leg(0, fwd_got, fwd_out, fwd_in, range(CHIPS))
    for index in (me, partner, above, below, above_p, below_p, far, far_p):
        arrived(1, index + 1 - 2 * core)

    def weigh(g):
        at2 = slice(g * 2 * TOK, (g + 1) * 2 * TOK)
        top = jnp.max(peak[at2], axis=1, keepdims=True)
        total[...] = jnp.zeros(total.shape, F32)
        mixed[...] = jnp.zeros(mixed.shape, F32)

        def chunk(n, carry):
            for b in (2 * n, 2 * n + 1):
                weights = jnp.exp2(scores[b, at2] - top)
                total[...] += weights[:, :HD] + weights[:, HD:]
                mixed[...] += dot(weights.astype(BF16), values[b])
            return carry

        lax.fori_loop(0, chip + 1, chunk, 0)
        ratio = mixed[...] / jnp.sum(total[...], axis=1, keepdims=True)
        taught[at2] = ratio.astype(BF16)

    def meet(g):
        for t in (2 * g, 2 * g + 1):
            at = slice(t * HD, (t + 1) * HD)
            entering = jnp.concatenate([fwd_in[0, t], fwd_in[1, t]], axis=0)
            sib = fwd_sibling[t]
            sib_state = jnp.concatenate([sib[0, 0:64], sib[1, 0:64]], axis=0)
            entering = jnp.where(
                core == 1, entering * jnp.exp(sib[0, 64:65]) + sib_state, entering
            )
            state_in[t] = entering
            sh, sl = halves(entering)
            starts = from_start[:, at]
            carried = (dot(r_ref[...], sh) + dot(r_ref[...], sl)) * starts
            residual = local_y[:, at] + carried - taught[t * TOK : (t + 1) * TOK].astype(F32)
            local_y[:, at] = residual
            wh, wl = halves(residual * starts)
            adjoint = dot(rt_buf[...], wh) + dot(rt_buf[...], wl)
            for half in range(2):
                bwd_local[t, half, 0:64] = adjoint[half * 64 : (half + 1) * 64]
                bwd_local[t, half, 64:72] = lane_decay[t]
        two = pl.ds(2 * g, 2)
        begin(
            remote(
                bwd_local.at[two],
                bwd_sibling.at[two],
                sib_send.at[3 + g],
                sib_recv.at[3 + g],
                "seq",
                sibling,
            )
        )

    def hand_over(g):
        two = pl.ds(2 * g, 2)
        remote(
            bwd_sibling.at[two],
            bwd_sibling.at[two],
            sib_send.at[3 + g],
            sib_recv.at[3 + g],
            "seq",
            sibling,
        ).wait_recv()
        for t in (2 * g, 2 * g + 1):
            chip_state(t, bwd_local, bwd_sibling, bwd_chip, False)
            send_leg(1, t, bwd_chip, bwd_got)

    def local_terms(t, carry):
        at = pl.ds(pl.multiple_of(t * HD, HD), HD)
        residual = local_y[:, at]
        xt = x_ref[:, at].T
        for side, own in ((0, first), (1, ~first)):
            rh, rl = halves(jnp.where(own, residual, 0.0))
            pair_buf[...] += decay_buf[2 * t + side] * (dot(rh, xt) + dot(rl, xt))
        return carry

    def back_terms(t, carry):
        at = pl.ds(pl.multiple_of(t * HD, HD), HD)
        residual_t = local_y[:, at].T
        rh, rl = halves(residual_t)
        pieces = []
        for side in range(2):
            own = slice(side * 64, (side + 1) * 64)
            both = jnp.concatenate([rh[own], rl[own]], axis=0)
            product = dot(both, mix_high[2 * t + side])
            pieces.append(product[0:64] + product[64:128] + dot(rh[own], mix_low[2 * t + side]))
        back[:, at] = jnp.concatenate(pieces, axis=0).T
        return carry

    def read_terms(t, carry):
        at = pl.ds(pl.multiple_of(t * HD, HD), HD)
        weighted = local_y[:, at] * from_start[:, at]
        sums[...] += three(dot_nt, weighted, state_in[t])
        return carry

    pair_buf[...] = jnp.zeros(pair_buf.shape, F32)
    sums[...] = jnp.zeros(sums.shape, F32)
    weigh(0)
    weigh(1)
    spread(0, fwd_in)
    weigh(2)
    spread_wait(0, fwd_in)
    meet(0)
    meet(1)
    hand_over(0)
    meet(2)
    hand_over(1)
    weigh(3)
    hand_over(2)
    meet(3)
    lax.fori_loop(0, 4, local_terms, 0)
    hand_over(3)
    lax.fori_loop(4, PAIRS, local_terms, 0)
    lax.fori_loop(0, PAIRS, read_terms, 0)
    ph, pw = halves(pair_buf[...])
    grad_read = sums[...] + dot(ph, w_ref[...]) + dot(pw, w_ref[...])
    th, tl = halves(pair_buf[...].T)
    grad_write = dot(th, r_ref[...]) + dot(tl, r_ref[...])
    for i in range(TP):
        early[i, 0:32] = grad_write[i * 32 : (i + 1) * 32]
        early[i, 32:64] = grad_read[i * 32 : (i + 1) * 32]

    def scatter(stage, source, got):
        got[tp] = source[tp]
        for hop in range(1, TP):
            to = lax.rem(tp + hop, TP)
            begin(
                remote(
                    source.at[to], got.at[tp], tp_send.at[stage, hop], tp_recv.at[stage, tp], "tp", to
                )
            )

    def gather(stage, source, got):
        got[tp] = source[...]
        for hop in range(1, TP):
            to = lax.rem(tp + hop, TP)
            begin(
                remote(source, got.at[tp], tp_send.at[stage, hop], tp_recv.at[stage, tp], "tp", to)
            )

    def collect(stage, got):
        for hop in range(1, TP):
            source = lax.rem(tp + hop, TP)
            remote(
                got.at[source],
                got.at[source],
                tp_send.at[stage, 0],
                tp_recv.at[stage, source],
                "tp",
                source,
            ).wait_recv()

    scatter(0, early, early_got)
    scan_leg(1, bwd_got, bwd_out, bwd_in, range(CHIPS - 1, -1, -1))
    lax.fori_loop(0, PAIRS, back_terms, 0)
    collect(0, early_got)
    acc = early_got[0]
    for i in range(1, TP):
        acc = acc + early_got[i]
    part[...] = acc
    gather(1, part.at[32:64], read_all)
    spread(1, bwd_in)
    spread_wait(1, bwd_in)

    def carry_terms(t, carry):
        at = pl.ds(pl.multiple_of(t * HD, HD), HD)
        arriving = jnp.concatenate([bwd_in[0, t], bwd_in[1, t]], axis=0)
        sib = bwd_sibling[t]
        sib_state = jnp.concatenate([sib[0, 0:64], sib[1, 0:64]], axis=0)
        arriving = jnp.where(
            core == 0, arriving * jnp.exp(sib[0, 64:65]) + sib_state, arriving
        )
        state_in[t] = arriving
        sums[...] += three(dot_nt, x_ref[:, at].astype(F32) * in_scale[:, at], arriving)
        return carry

    sums[...] = jnp.zeros(sums.shape, F32)
    lax.fori_loop(0, PAIRS, carry_terms, 0)
    for i in range(TP):
        late[i] = sums[i * 32 : (i + 1) * 32]
    scatter(2, late, late_got)

    row16 = lax.broadcasted_iota(jnp.int32, (16, HD), 0)
    lane16 = lax.broadcasted_iota(jnp.int32, (16, HD), 1)
    gls_ref[...] = jnp.zeros(gls_ref.shape, F32)

    def store_of(t):
        at = pl.ds(pl.multiple_of(t * HD, HD), HD)
        return pltpu.make_async_copy(back.at[:, at], gi_hbm.at[:, at], out_sem.at[t])

    def finish(t, carry):
        at = pl.ds(pl.multiple_of(t * HD, HD), HD)
        ah, al = halves(state_in[t])
        grad = back[:, at] + in_scale[:, at] * (dot(w_ref[...], ah) + dot(w_ref[...], al))
        back[:, at] = grad
        store_of(t).start()
        gh, gl = halves(x_ref[:, at].astype(F32) * grad)
        pick = jnp.where(row16 == 2 * t + lane16 // 64, 1.0, 0.0).astype(BF16)
        gls_ref[...] += dot_nt(pick, gh) + dot_nt(pick, gl)
        return carry

    lax.fori_loop(0, PAIRS, finish, 0)
    collect(1, read_all)
    for i in range(TP):
        gr_ref[i * 32 : (i + 1) * 32] = read_all[i]
    collect(2, late_got)
    acc = part[0:32]
    for i in range(TP):
        acc = acc + late_got[i]
    write_part[...] = acc
    gather(3, write_part, write_all)
    for t in range(PAIRS):
        store_of(t).wait()
    for copy in started:
        copy.wait_send()
    for t in range(PAIRS):

        @pl.when(chip != t)
        def _():
            leg(0, t, fwd_chip, fwd_got).wait_send()
            leg(1, t, bwd_chip, bwd_got).wait_send()

    collect(3, write_all)
    for i in range(TP):
        gw_ref[i * 32 : (i + 1) * 32] = write_all[i]


def on_device(
    query_rows, key_rows, value_rows, mixer_input, write_rows, read_rows, log_step, log_decay
):
    dma = pltpu.SemaphoreType.DMA
    packet = (PAIRS, 2, 72, HD)
    exchange = [
        pltpu.VMEM(packet, F32),
        pltpu.VMEM(packet, F32),
        pltpu.VMEM((PAIRS, 72, HD), F32),
        pltpu.VMEM((CHIPS, 72, HD), F32),
        pltpu.VMEM((CHIPS, 64, HD), F32),
        pltpu.VMEM((2, PAIRS, 64, HD), F32),
    ]
    whole = pl.BlockSpec(memory_space=pl.ANY)
    vmem = pl.BlockSpec(memory_space=pltpu.VMEM)
    wide = (TOK, PAIRS * HD)
    share = (TP, 32, HD)
    return pl.pallas_call(
        main_kernel,
        out_shape=(
            jax.ShapeDtypeStruct(wide, F32),
            jax.ShapeDtypeStruct((TOK, HD), F32),
            jax.ShapeDtypeStruct((TOK, HD), F32),
            jax.ShapeDtypeStruct((2 * PAIRS, TOK), F32),
        ),
        in_specs=[whole] * 8,
        out_specs=(whole, vmem, vmem, vmem),
        scratch_shapes=[
            pltpu.VMEM(wide, BF16),
            pltpu.VMEM(wide, BF16),
            pltpu.VMEM((TOK, HD), BF16),
            pltpu.VMEM((TOK, HD), BF16),
            pltpu.VMEM((2 * PAIRS, TOK), F32),
            pltpu.VMEM((2 * PAIRS, TOK), F32),
            pltpu.VMEM((SEQ, TOK, HD), BF16),
            pltpu.VMEM((SEQ, TOK, HD), BF16),
            pltpu.VMEM((SEQ, 8 * TOK, TOK), F32),
            pltpu.VMEM((8 * TOK, HD), F32),
            pltpu.VMEM((2 * TOK, HD), F32),
            pltpu.VMEM((2 * TOK, HD), F32),
            pltpu.VMEM((8 * TOK, HD), BF16),
            pltpu.VMEM((16, TOK, TOK), F32),
            pltpu.VMEM((16, TOK, TOK), BF16),
            pltpu.VMEM((16, TOK, TOK), BF16),
            pltpu.VMEM(wide, F32),
            pltpu.VMEM(wide, F32),
            pltpu.VMEM(wide, F32),
            pltpu.VMEM(wide, F32),
            pltpu.VMEM((HD, TOK), BF16),
            pltpu.VMEM((HD, TOK), BF16),
            pltpu.VMEM((TOK, TOK), F32),
            pltpu.VMEM((TOK, HD), F32),
            pltpu.VMEM((PAIRS, 8, HD), F32),
            *exchange,
            pltpu.VMEM((PAIRS, HD, HD), F32),
            *exchange,
            pltpu.VMEM((TP, 64, HD), F32),
            pltpu.VMEM((TP, 64, HD), F32),
            pltpu.VMEM((64, HD), F32),
            pltpu.VMEM(share, F32),
            pltpu.VMEM(share, F32),
            pltpu.VMEM(share, F32),
            pltpu.VMEM((32, HD), F32),
            pltpu.VMEM(share, F32),
            dma((8,)),
            dma((PAIRS,)),
            dma((16,)),
            dma((SEQ,)),
            dma((16,)),
            dma((SEQ,)),
            dma((8,)),
            dma((8,)),
            dma((2, CHIPS)),
            dma((2, CHIPS)),
            dma((2, CHIPS)),
            dma((2, CHIPS)),
            dma((4, TP)),
            dma((4, TP)),
        ],
        compiler_params=pltpu.CompilerParams(
            collective_id=0, has_side_effects=True, vmem_limit_bytes=61 * 1024 * 1024
        ),
        name="distill",
    )(query_rows, key_rows, value_rows, mixer_input, write_rows, read_rows, log_step, log_decay)


def solution(mesh):
    in_specs = (
        P("seq", "tp"),
        P("seq", "tp"),
        P("seq", "tp"),
        P("seq", "tp"),
        P("seq", None),
        P("seq", None),
        P("tp", "seq"),
        P("tp", "seq"),
    )
    out_specs = (P("seq", "tp"), P("seq", None), P("seq", None), P("tp", "seq"))
    return jax.shard_map(
        on_device, mesh=mesh, in_specs=in_specs, out_specs=out_specs, check_vma=False
    )
```

time: 89.4 us -> 72 us (0.81)
  Pallas kernels: 83.2 us -> 66.5 us
    pallas_call x2 -> x1, Pallas kernels: 83.2 us -> 66.5 us  [on_device(): pl.pallas_call(main_kernel, out_shape=(jax.ShapeDtypeStruct(wide, F32), j...]
    reshape x1 -> x0, local copies, waits for them, and re-layouts: 1.34 us -> none  [on_device(): grad_step.reshape(2 * PAIRS, TOK)]
    unnamed x7 -> x10, local copies, waits for them, and re-layouts: 3.95 us -> 4.62 us
where the time goes in v2:
time: 72 us; the launch traced here: 71.8 us
  Pallas kernels  66.5 us (92%)
  local copies, waits for them, and re-layouts  4.62 us (6%)
    pallas_call x1, Pallas kernels, on_device(): pl.pallas_call(main_kernel, out_shape=(jax.ShapeDtypeStruct(wide, F32), j...  66.5 us
    unnamed x10, local copies, waits for them, and re-layouts  4.62 us

profile of v2, /device:TPU:0, one launch (start us, length us, event | category | flops | bytes accessed | tf_op | source)
XLA Modules:
  0.0 71.8 jit_solution(11857459990858482121)
XLA Ops:
  0.6 66.5 %distill.1 = (f32[256,1024]{1,0:T(8,128)}, f32[256,128]{1,0:T(8,128)}, f32[256,128]{1,0:T(8,128)}, f32[16,256]{1,0:T(8,128)}) custom-call(bf16[256,1024]{1,0:T(8,128)(2,1)} %q_hbm.1, bf16[256,128]{1,0:T(8,128)(2,1)} %k_hbm.1, bf16[256,128]{1,0:T(8,128)(2,1)} %v_hbm.1, bf16[256,1024]{1,0:T(8,128)(2,1)} %x_hbm.1, bf16[256,128]{1,0:T(8,128)(2,1)} %w_hbm.1, ...), custom_call_target="tpu_custom_call" | custom-call | tf_op jit(solution)/shard_map/distill/pallas_call | solution.py:676
  67.2 0.0 copy-start.1
  67.2 2.3 %copy.16 = f32[256,1024]{1,0:T(8,128)} copy(f32[256,1024]{1,0:T(8,128)} %get-tuple-element.8) | data formatting | bytes 2097152
  69.5 0.0 copy-done.1
  69.5 0.0 copy-start
  69.5 0.7 copy.17
  70.2 0.3 copy-done
  70.5 0.0 copy-start.2
  70.5 0.7 copy.18
  71.1 0.1 copy-done.2
  71.2 0.6 copy.19
Async XLA Ops:
  67.2 2.4 %copy-start.1 = (f32[256,128]{1,0:T(8,128)S(1)}, f32[256,128]{1,0:T(8,128)}, u32[]{:S(2)}) copy-start(f32[256,128]{1,0:T(8,128)} %get-tuple-element.9) | copy-start | bytes 393220
  69.5 1.0 %copy-start = (f32[256,128]{1,0:T(8,128)S(1)}, f32[256,128]{1,0:T(8,128)}, u32[]{:S(2)}) copy-start(f32[256,128]{1,0:T(8,128)} %get-tuple-element.10) | copy-start | bytes 393220
  70.5 0.7 copy-start.2

commit v3 on v2

--- a/solution.py
+++ b/solution.py
@@ -58,7 +58,7 @@
     r_hbm,
     ls_hbm,
     ld_hbm,
-    gi_hbm,
+    back,
     gw_ref,
     gr_ref,
     gls_ref,
@@ -81,7 +81,6 @@
     from_start,
     in_scale,
     local_y,
-    back,
     wt_buf,
     rt_buf,
     pair_buf,
@@ -109,7 +108,6 @@
     write_part,
     write_all,
     in_sem,
-    out_sem,
     key_send,
     key_recv,
     value_send,
@@ -354,6 +352,12 @@
             sibling,
         ).wait_recv()
 
+    remote(
+        fwd_sibling, fwd_sibling, sib_send.at[0], sib_recv.at[0], "seq", sibling
+    ).wait_recv()
+    for t in range(PAIRS):
+        chip_state(t, fwd_local, fwd_sibling, fwd_chip, True)
+        send_leg(0, t, fwd_chip, fwd_got)
     for h in range(8):
         build(h)
     relay_one(1)
@@ -372,6 +376,22 @@
             scores[b, at] = s
             peak[at] = jnp.maximum(peak[at], jnp.maximum(s[:, :HD], s[:, HD:]))
 
+    def score_other(shift):
+        other = lax.rem(row + shift, 4)
+
+        def step(i, carry):
+            base = other * 4 + lax.rem(plane + i, 2) * 2
+            arrived(0, base + 1 - core)
+
+            @pl.when(other < row)
+            def _():
+                score_block(base, False)
+                score_block(base + 1, False)
+
+            return carry
+
+        lax.fori_loop(0, 2, step, 0)
+
     def score_row(shift, low):
         def step(i, carry):
             flip = lax.rem(i, 2)
@@ -395,23 +415,20 @@
 
     score_block(me, True)
 
-    @pl.when(core == 0)
-    def _():
-        scores[me + 1] = jnp.full((8 * TOK, TOK), LOW, F32)
+    def blank(b, carry):
+        scores[b] = jnp.full((8 * TOK, TOK), LOW, F32)
+        return carry
+
+    lax.fori_loop(me + 1, 4 * row + 4, blank, 0)
 
     for h in range(8, 16):
         build(h)
     score_row(0, 1)
     relay_two(1)
     relay_three(0)
-    remote(
-        fwd_sibling, fwd_sibling, sib_send.at[0], sib_recv.at[0], "seq", sibling
-    ).wait_recv()
-    for t in range(PAIRS):
-        chip_state(t, fwd_local, fwd_sibling, fwd_chip, True)
-        send_leg(0, t, fwd_chip, fwd_got)
-    score_row(3, 0)
-    score_row(1, 0)
+    score_other(3)
+    scan_leg(0, fwd_got, fwd_out, fwd_in, range(CHIPS))
+    score_other(1)
     relay_three(1)
 
     def make_y(t, carry):
@@ -428,8 +445,7 @@
         return carry
 
     lax.fori_loop(0, PAIRS, make_y, 0)
-    score_row(2, 0)
-    scan_leg(0, fwd_got, fwd_out, fwd_in, range(CHIPS))
+    score_other(2)
     for index in (me, partner, above, below, above_p, below_p, far, far_p):
         arrived(1, index + 1 - 2 * core)
 
@@ -440,13 +456,18 @@
         mixed[...] = jnp.zeros(mixed.shape, F32)
 
         def chunk(n, carry):
-            for b in (2 * n, 2 * n + 1):
-                weights = jnp.exp2(scores[b, at2] - top)
-                total[...] += weights[:, :HD] + weights[:, HD:]
-                mixed[...] += dot(weights.astype(BF16), values[b])
+            low, folded = [], None
+            for b in range(4):
+                weights = jnp.exp2(scores[4 * n + b, at2] - top)
+                low.append(weights.astype(BF16))
+                both = weights[:, :HD] + weights[:, HD:]
+                folded = both if folded is None else folded + both
+            total[...] += folded
+            shown = values[pl.ds(4 * n, 4)].reshape(4 * TOK, HD)
+            mixed[...] += dot(jnp.concatenate(low, axis=1), shown)
             return carry
 
-        lax.fori_loop(0, chip + 1, chunk, 0)
+        lax.fori_loop(0, row + 1, chunk, 0)
         ratio = mixed[...] / jnp.sum(total[...], axis=1, keepdims=True)
         taught[at2] = ratio.astype(BF16)
 
@@ -615,16 +636,11 @@
     lane16 = lax.broadcasted_iota(jnp.int32, (16, HD), 1)
     gls_ref[...] = jnp.zeros(gls_ref.shape, F32)
 
-    def store_of(t):
-        at = pl.ds(pl.multiple_of(t * HD, HD), HD)
-        return pltpu.make_async_copy(back.at[:, at], gi_hbm.at[:, at], out_sem.at[t])
-
     def finish(t, carry):
         at = pl.ds(pl.multiple_of(t * HD, HD), HD)
         ah, al = halves(state_in[t])
         grad = back[:, at] + in_scale[:, at] * (dot(w_ref[...], ah) + dot(w_ref[...], al))
         back[:, at] = grad
-        store_of(t).start()
         gh, gl = halves(x_ref[:, at].astype(F32) * grad)
         pick = jnp.where(row16 == 2 * t + lane16 // 64, 1.0, 0.0).astype(BF16)
         gls_ref[...] += dot_nt(pick, gh) + dot_nt(pick, gl)
@@ -640,8 +656,6 @@
         acc = acc + late_got[i]
     write_part[...] = acc
     gather(3, write_part, write_all)
-    for t in range(PAIRS):
-        store_of(t).wait()
     for copy in started:
         copy.wait_send()
     for t in range(PAIRS):
@@ -654,6 +668,17 @@
     collect(3, write_all)
     for i in range(TP):
         gw_ref[i * 32 : (i + 1) * 32] = write_all[i]
+
+
+def write_kernel(*refs):
+    copies = [
+        pltpu.make_async_copy(src, dst, refs[8].at[n])
+        for n, (src, dst) in enumerate(zip(refs[0:4], refs[4:8]))
+    ]
+    for copy in copies:
+        copy.start()
+    for copy in copies:
+        copy.wait()
 
 
 def on_device(
@@ -673,16 +698,16 @@
     vmem = pl.BlockSpec(memory_space=pltpu.VMEM)
     wide = (TOK, PAIRS * HD)
     share = (TP, 32, HD)
-    return pl.pallas_call(
+    held = pl.pallas_call(
         main_kernel,
         out_shape=(
-            jax.ShapeDtypeStruct(wide, F32),
-            jax.ShapeDtypeStruct((TOK, HD), F32),
-            jax.ShapeDtypeStruct((TOK, HD), F32),
-            jax.ShapeDtypeStruct((2 * PAIRS, TOK), F32),
+            pltpu.VMEM(wide, F32),
+            pltpu.VMEM((TOK, HD), F32),
+            pltpu.VMEM((TOK, HD), F32),
+            pltpu.VMEM((2 * PAIRS, TOK), F32),
         ),
         in_specs=[whole] * 8,
-        out_specs=(whole, vmem, vmem, vmem),
+        out_specs=(vmem,) * 4,
         scratch_shapes=[
             pltpu.VMEM(wide, BF16),
             pltpu.VMEM(wide, BF16),
@@ -703,7 +728,6 @@
             pltpu.VMEM(wide, F32),
             pltpu.VMEM(wide, F32),
             pltpu.VMEM(wide, F32),
-            pltpu.VMEM(wide, F32),
             pltpu.VMEM((HD, TOK), BF16),
             pltpu.VMEM((HD, TOK), BF16),
             pltpu.VMEM((TOK, TOK), F32),
@@ -721,7 +745,6 @@
             pltpu.VMEM((32, HD), F32),
             pltpu.VMEM(share, F32),
             dma((8,)),
-            dma((PAIRS,)),
             dma((16,)),
             dma((SEQ,)),
             dma((16,)),
@@ -740,6 +763,20 @@
         ),
         name="distill",
     )(query_rows, key_rows, value_rows, mixer_input, write_rows, read_rows, log_step, log_decay)
+    return pl.pallas_call(
+        write_kernel,
+        out_shape=(
+            jax.ShapeDtypeStruct(wide, F32),
+            jax.ShapeDtypeStruct((TOK, HD), F32),
+            jax.ShapeDtypeStruct((TOK, HD), F32),
+            jax.ShapeDtypeStruct((2 * PAIRS, TOK), F32),
+        ),
+        in_specs=[vmem] * 4,
+        out_specs=(whole,) * 4,
+        scratch_shapes=[dma((4,))],
+        compiler_params=pltpu.CompilerParams(vmem_limit_bytes=1024 * 1024),
+        name="store",
+    )(*held)
 
 
 def solution(mesh):

time: 72 us -> 65.5 us (0.910)
  local copies, waits for them, and re-layouts: 4.62 us -> 0 us
  Pallas kernels: 66.5 us -> 64.4 us
    unnamed x10 -> x0, local copies, waits for them, and re-layouts: 4.62 us -> none
    pallas_call x1 -> x2, Pallas kernels: 66.5 us -> 64.4 us  [the longest x1 63.3 us: on_device(): pl.pallas_call(main_kernel, out_shape=(pltpu.VMEM(wide, F32), pltpu.VMEM(...]
where the time goes in v3:
time: 65.5 us; the launch traced here: 65 us
  Pallas kernels  64.4 us (98%)
    pallas_call x1, Pallas kernels, on_device(): pl.pallas_call(main_kernel, out_shape=(pltpu.VMEM(wide, F32), pltpu.VMEM(...  63.3 us

profile of v3, /device:TPU:0, one launch (start us, length us, event | category | flops | bytes accessed | tf_op | source)
XLA Modules:
  0.0 65.0 jit_solution(17282525845040567647)
XLA Ops:
  0.6 63.3 %distill.1 = (f32[256,1024]{1,0:T(8,128)S(1)}, f32[256,128]{1,0:T(8,128)S(1)}, f32[256,128]{1,0:T(8,128)S(1)}, f32[16,256]{1,0:T(8,128)S(1)}) custom-call(bf16[256,1024]{1,0:T(8,128)(2,1)} %q_hbm.1, bf16[256,128]{1,0:T(8,128)(2,1)} %k_hbm.1, bf16[256,128]{1,0:T(8,128)(2,1)} %v_hbm.1, bf16[256,1024]{1,0:T(8,128)(2,1)} %x_hbm.1, bf16[256,128]{1,0:T(8,128)(2,1)} %w_hbm.1, ...), custom_call_target="tpu_custom_call" | custom-call | tf_op jit(solution)/shard_map/distill/pallas_call | solution.py:701
  64.0 1.1 %store.1 = (f32[256,1024]{1,0:T(8,128)}, f32[256,128]{1,0:T(8,128)}, f32[256,128]{1,0:T(8,128)}, f32[16,256]{1,0:T(8,128)}) custom-call(f32[256,1024]{1,0:T(8,128)S(1)} %get-tuple-element.8.refs_0_, f32[256,128]{1,0:T(8,128)S(1)} %get-tuple-element.9.refs_1_, f32[256,128]{1,0:T(8,128)S(1)} %get-tuple-element.10.refs_2_, f32[16,256]{1,0:T(8,128)S(1)} %get-tuple-element.11.refs_3_), custom_call_target="tpu_custom_call" | custom-call | tf_op jit(solution)/shard_map/store/pallas_call | solution.py:766

commit v4 on v3

--- a/solution.py
+++ b/solution.py
@@ -85,7 +85,6 @@
     rt_buf,
     pair_buf,
     sums,
-    lane_decay,
     fwd_local,
     fwd_sibling,
     fwd_chip,
@@ -231,25 +230,34 @@
     lane = lax.broadcasted_iota(jnp.int32, (TOK, HD), 1)
     first = lane < 64
     lane8 = lax.broadcasted_iota(jnp.int32, (8, HD), 1)
+
+    def fwd_piece(g):
+        two = pl.ds(2 * g, 2)
+        return remote(
+            fwd_local.at[two],
+            fwd_sibling.at[two],
+            sib_send.at[7 + g],
+            sib_recv.at[7 + g],
+            "seq",
+            sibling,
+        )
+
     wt_buf[...] = w_ref[...].T
     for t in range(PAIRS):
         a, b = 2 * t, 2 * t + 1
         at = slice(t * HD, (t + 1) * HD)
-        from_start[:, at] = jnp.exp(
-            jnp.where(first, columns[:, a : a + 1], columns[:, b : b + 1])
-        )
         scale = jnp.exp(
             jnp.where(first, columns[:, 16 + a : 17 + a], columns[:, 16 + b : 17 + b])
         )
         in_scale[:, at] = scale
         tile = jnp.where(lane8 < 64, end[a : a + 1, :], end[b : b + 1, :])
-        lane_decay[t] = tile
         high, low = halves(x_ref[:, at].astype(F32) * scale)
         state = dot(wt_buf[...], high) + dot(wt_buf[...], low)
         for half in range(2):
             fwd_local[t, half, 0:64] = state[half * 64 : (half + 1) * 64]
             fwd_local[t, half, 64:72] = tile
-    begin(remote(fwd_local, fwd_sibling, sib_send.at[0], sib_recv.at[0], "seq", sibling))
+        if t % 2:
+            begin(fwd_piece(t // 2))
     loads[6].wait()
     rt_buf[...] = r_ref[...].T
     inner = dot_nt(r_ref[...], w_ref[...])
@@ -268,7 +276,9 @@
         early_core = jnp.where(core == 0, mine, other)
         late_core = jnp.where(core == 0, other, mine)
         if not early_first:
-            early_core, late_core = late_core, early_core
+            span = jnp.where(core == 0, fwd_local[t, 0, 64:65], fwd_sibling[t, 0, 64:65])
+            out[t] = late_core * jnp.exp(span) + early_core
+            return
         out[t, 0:64] = early_core[0:64] * jnp.exp(late_core[64:65]) + late_core[0:64]
         out[t, 64:72] = early_core[64:72] + late_core[64:72]
 
@@ -305,7 +315,7 @@
         running = jnp.zeros((64, HD), F32)
         for i in order:
             out[i] = running
-            running = running * jnp.exp(got[i, 64:65]) + got[i, 0:64]
+            running = running * jnp.exp(fwd_got[i, 64:65]) + got[i, 0:64]
         into[core, chip] = out[chip]
         for hop in range(1, CHIPS):
             target = lax.rem(chip + hop, CHIPS)
@@ -352,12 +362,16 @@
             sibling,
         ).wait_recv()
 
-    remote(
-        fwd_sibling, fwd_sibling, sib_send.at[0], sib_recv.at[0], "seq", sibling
-    ).wait_recv()
+    for g in range(4):
+        fwd_piece(g).wait_recv()
+        for t in (2 * g, 2 * g + 1):
+            chip_state(t, fwd_local, fwd_sibling, fwd_chip, True)
+            send_leg(0, t, fwd_chip, fwd_got)
     for t in range(PAIRS):
-        chip_state(t, fwd_local, fwd_sibling, fwd_chip, True)
-        send_leg(0, t, fwd_chip, fwd_got)
+        a, b = 2 * t, 2 * t + 1
+        from_start[:, t * HD : (t + 1) * HD] = jnp.exp(
+            jnp.where(first, columns[:, a : a + 1], columns[:, b : b + 1])
+        )
     for h in range(8):
         build(h)
     relay_one(1)
@@ -489,8 +503,7 @@
             wh, wl = halves(residual * starts)
             adjoint = dot(rt_buf[...], wh) + dot(rt_buf[...], wl)
             for half in range(2):
-                bwd_local[t, half, 0:64] = adjoint[half * 64 : (half + 1) * 64]
-                bwd_local[t, half, 64:72] = lane_decay[t]
+                bwd_local[t, half] = adjoint[half * 64 : (half + 1) * 64]
         two = pl.ds(2 * g, 2)
         begin(
             remote(
@@ -567,10 +580,9 @@
     ph, pw = halves(pair_buf[...])
     grad_read = sums[...] + dot(ph, w_ref[...]) + dot(pw, w_ref[...])
     th, tl = halves(pair_buf[...].T)
-    grad_write = dot(th, r_ref[...]) + dot(tl, r_ref[...])
+    sums[...] = dot(th, r_ref[...]) + dot(tl, r_ref[...])
     for i in range(TP):
-        early[i, 0:32] = grad_write[i * 32 : (i + 1) * 32]
-        early[i, 32:64] = grad_read[i * 32 : (i + 1) * 32]
+        early[i] = grad_read[i * 32 : (i + 1) * 32]
 
     def scatter(stage, source, got):
         got[tp] = source[tp]
@@ -610,23 +622,44 @@
     for i in range(1, TP):
         acc = acc + early_got[i]
     part[...] = acc
-    gather(1, part.at[32:64], read_all)
-    spread(1, bwd_in)
-    spread_wait(1, bwd_in)
-
-    def carry_terms(t, carry):
+    gather(1, part, read_all)
+
+    def across(t, half):
+        return remote(
+            bwd_in.at[half, t],
+            bwd_in.at[half, t],
+            sib_send.at[11 + t],
+            sib_recv.at[11 + t],
+            "seq",
+            sibling,
+        )
+
+    begin(across(chip, core))
+    for hop in range(1, CHIPS):
+        source = lax.rem(chip + hop, CHIPS)
+        remote(
+            bwd_in.at[core, source],
+            bwd_in.at[core, source],
+            ret_send.at[1, 0],
+            ret_recv.at[1, source],
+            "seq",
+            sibling,
+        ).wait_recv()
+        begin(across(source, core))
+
+    def carry_terms(i, carry):
+        t = lax.rem(chip + i, CHIPS)
+        across(t, 1 - core).wait_recv()
         at = pl.ds(pl.multiple_of(t * HD, HD), HD)
         arriving = jnp.concatenate([bwd_in[0, t], bwd_in[1, t]], axis=0)
-        sib = bwd_sibling[t]
-        sib_state = jnp.concatenate([sib[0, 0:64], sib[1, 0:64]], axis=0)
+        sib_state = jnp.concatenate([bwd_sibling[t, 0], bwd_sibling[t, 1]], axis=0)
         arriving = jnp.where(
-            core == 0, arriving * jnp.exp(sib[0, 64:65]) + sib_state, arriving
+            core == 0, arriving * jnp.exp(fwd_sibling[t, 0, 64:65]) + sib_state, arriving
         )
         state_in[t] = arriving
         sums[...] += three(dot_nt, x_ref[:, at].astype(F32) * in_scale[:, at], arriving)
         return carry
 
-    sums[...] = jnp.zeros(sums.shape, F32)
     lax.fori_loop(0, PAIRS, carry_terms, 0)
     for i in range(TP):
         late[i] = sums[i * 32 : (i + 1) * 32]
@@ -651,8 +684,8 @@
     for i in range(TP):
         gr_ref[i * 32 : (i + 1) * 32] = read_all[i]
     collect(2, late_got)
-    acc = part[0:32]
-    for i in range(TP):
+    acc = late_got[0]
+    for i in range(1, TP):
         acc = acc + late_got[i]
     write_part[...] = acc
     gather(3, write_part, write_all)
@@ -732,13 +765,17 @@
             pltpu.VMEM((HD, TOK), BF16),
             pltpu.VMEM((TOK, TOK), F32),
             pltpu.VMEM((TOK, HD), F32),
-            pltpu.VMEM((PAIRS, 8, HD), F32),
             *exchange,
             pltpu.VMEM((PAIRS, HD, HD), F32),
-            *exchange,
-            pltpu.VMEM((TP, 64, HD), F32),
-            pltpu.VMEM((TP, 64, HD), F32),
-            pltpu.VMEM((64, HD), F32),
+            pltpu.VMEM((PAIRS, 2, 64, HD), F32),
+            pltpu.VMEM((PAIRS, 2, 64, HD), F32),
+            pltpu.VMEM((PAIRS, 64, HD), F32),
+            pltpu.VMEM((CHIPS, 64, HD), F32),
+            pltpu.VMEM((CHIPS, 64, HD), F32),
+            pltpu.VMEM((2, PAIRS, 64, HD), F32),
+            pltpu.VMEM(share, F32),
+            pltpu.VMEM(share, F32),
+            pltpu.VMEM((32, HD), F32),
             pltpu.VMEM(share, F32),
             pltpu.VMEM(share, F32),
             pltpu.VMEM(share, F32),
@@ -749,8 +786,8 @@
             dma((SEQ,)),
             dma((16,)),
             dma((SEQ,)),
-            dma((8,)),
-            dma((8,)),
+            dma((19,)),
+            dma((19,)),
             dma((2, CHIPS)),
             dma((2, CHIPS)),
             dma((2, CHIPS)),

time: 65.5 us -> 64.3 us (0.982)
  Pallas kernels: 64.4 us -> 63.6 us
    pallas_call x1, Pallas kernels: 63.3 us -> 62.5 us  [on_device(): pl.pallas_call(main_kernel, out_shape=(pltpu.VMEM(wide, F32), pltpu.VMEM(...]
where the time goes in v4:
time: 64.3 us; the launch traced here: 64.2 us
  Pallas kernels  63.6 us (99%)
    pallas_call x1, Pallas kernels, on_device(): pl.pallas_call(main_kernel, out_shape=(pltpu.VMEM(wide, F32), pltpu.VMEM(...  62.5 us

profile of v4, /device:TPU:0, one launch (start us, length us, event | category | flops | bytes accessed | tf_op | source)
XLA Modules:
  0.0 64.2 jit_solution(11048521793439046158)
XLA Ops:
  0.6 62.5 %distill.1 = (f32[256,1024]{1,0:T(8,128)S(1)}, f32[256,128]{1,0:T(8,128)S(1)}, f32[256,128]{1,0:T(8,128)S(1)}, f32[16,256]{1,0:T(8,128)S(1)}) custom-call(bf16[256,1024]{1,0:T(8,128)(2,1)} %q_hbm.1, bf16[256,128]{1,0:T(8,128)(2,1)} %k_hbm.1, bf16[256,128]{1,0:T(8,128)(2,1)} %v_hbm.1, bf16[256,1024]{1,0:T(8,128)(2,1)} %x_hbm.1, bf16[256,128]{1,0:T(8,128)(2,1)} %w_hbm.1, ...), custom_call_target="tpu_custom_call" | custom-call | tf_op jit(solution)/shard_map/distill/pallas_call | solution.py:734
  63.1 1.1 %store.1 = (f32[256,1024]{1,0:T(8,128)}, f32[256,128]{1,0:T(8,128)}, f32[256,128]{1,0:T(8,128)}, f32[16,256]{1,0:T(8,128)}) custom-call(f32[256,1024]{1,0:T(8,128)S(1)} %get-tuple-element.8.refs_0_, f32[256,128]{1,0:T(8,128)S(1)} %get-tuple-element.9.refs_1_, f32[256,128]{1,0:T(8,128)S(1)} %get-tuple-element.10.refs_2_, f32[16,256]{1,0:T(8,128)S(1)} %get-tuple-element.11.refs_3_), custom_call_target="tpu_custom_call" | custom-call | tf_op jit(solution)/shard_map/store/pallas_call | solution.py:803

commit v5 on v4

--- a/solution.py
+++ b/solution.py
@@ -550,6 +550,9 @@
             product = dot(both, mix_high[2 * t + side])
             pieces.append(product[0:64] + product[64:128] + dot(rh[own], mix_low[2 * t + side]))
         back[:, at] = jnp.concatenate(pieces, axis=0).T
+        high, low = halves(x_ref[:, at].astype(F32) * in_scale[:, at])
+        q_ref[:, at] = high
+        taught[pl.ds(pl.multiple_of(t * TOK, TOK), TOK)] = low
         return carry
 
     def read_terms(t, carry):
@@ -657,7 +660,9 @@
             core == 0, arriving * jnp.exp(fwd_sibling[t, 0, 64:65]) + sib_state, arriving
         )
         state_in[t] = arriving
-        sums[...] += three(dot_nt, x_ref[:, at].astype(F32) * in_scale[:, at], arriving)
+        ah, al = halves(arriving)
+        high, low = q_ref[:, at], taught[pl.ds(pl.multiple_of(t * TOK, TOK), TOK)]
+        sums[...] += dot_nt(high, ah) + dot_nt(low, ah) + dot_nt(high, al)
         return carry
 
     lax.fori_loop(0, PAIRS, carry_terms, 0)

time: 64.3 us -> 64.3 us (level)
  no operation moved by 1% of the time
where the time goes in v5:
time: 64.3 us; the launch traced here: 64.2 us
  Pallas kernels  63.5 us (99%)
    pallas_call x1, Pallas kernels, on_device(): pl.pallas_call(main_kernel, out_shape=(pltpu.VMEM(wide, F32), pltpu.VMEM(...  62.5 us

profile of v5, /device:TPU:0, one launch (start us, length us, event | category | flops | bytes accessed | tf_op | source)
XLA Modules:
  0.0 64.2 jit_solution(12467303318145038876)
XLA Ops:
  0.6 62.5 %distill.1 = (f32[256,1024]{1,0:T(8,128)S(1)}, f32[256,128]{1,0:T(8,128)S(1)}, f32[256,128]{1,0:T(8,128)S(1)}, f32[16,256]{1,0:T(8,128)S(1)}) custom-call(bf16[256,1024]{1,0:T(8,128)(2,1)} %q_hbm.1, bf16[256,128]{1,0:T(8,128)(2,1)} %k_hbm.1, bf16[256,128]{1,0:T(8,128)(2,1)} %v_hbm.1, bf16[256,1024]{1,0:T(8,128)(2,1)} %x_hbm.1, bf16[256,128]{1,0:T(8,128)(2,1)} %w_hbm.1, ...), custom_call_target="tpu_custom_call" | custom-call | tf_op jit(solution)/shard_map/distill/pallas_call | solution.py:739
  63.1 1.1 %store.1 = (f32[256,1024]{1,0:T(8,128)}, f32[256,128]{1,0:T(8,128)}, f32[256,128]{1,0:T(8,128)}, f32[16,256]{1,0:T(8,128)}) custom-call(f32[256,1024]{1,0:T(8,128)S(1)} %get-tuple-element.8.refs_0_, f32[256,128]{1,0:T(8,128)S(1)} %get-tuple-element.9.refs_1_, f32[256,128]{1,0:T(8,128)S(1)} %get-tuple-element.10.refs_2_, f32[16,256]{1,0:T(8,128)S(1)} %get-tuple-element.11.refs_3_), custom_call_target="tpu_custom_call" | custom-call | tf_op jit(solution)/shard_map/store/pallas_call | solution.py:808
